TPU v7x, 128 devices: a whole 4x4x4 slice. The times are simulated.
128 devices in a mesh: row: 8 (over z, core), col: 4 (over y), rhs: 4 (over x).
Axes of the slice: x: 4, y: 4, z: 4, core: 2. Of those that a mesh axis runs over, the one named last changes fastest.
Arguments:
- right_side: float32 [8, 64, 8192], P('row', 'rhs', 'col'), may hold values from -6 to 6
- guess: float32 [8, 64, 8192], P('row', 'rhs', 'col'), may hold values from -6 to 6
- inverse: bfloat16 [8, 8192, 8192], P('row', 'rhs', 'col'), may hold values from -0.0625 to 0.0625
- left_factor: bfloat16 [8, 8, 64, 8192], P('row', None, None, 'col'), may hold values from -0.25 to 0.25
- right_factor: bfloat16 [8, 8, 64, 8192], P('row', None, None, 'col'), may hold values from -0.0625 to 0.0625
- ranks: int32 [8, 8], replicated, may hold values from 16 to 64
Outputs:
- solution: float32 [8, 64, 8192], P('row', 'rhs', 'col')
Inputs may be any that keep to these rules, and one draw needn't show every extreme that they name: ranks[i, j] is the rank of the block in block row i and block column j; diagonal entries are not read.
All inputs are finite; a program needn't handle non-finite values.
Results may differ from a plain program's by a relative error of at most 0.008.
Values may be sent and summed in bfloat16 or wider, within the bound.
No kernel may reach another device: no remote copies, remote signals or barrier semaphores. Data moves between devices by JAX's collectives and lax.ppermute only.
A program may use at most 128 MiB of HBM per device.

v0:
```python
import numpy as np

import jax
import jax.numpy as jnp
from jax import lax
from jax.experimental import pallas as pl
from jax.experimental.pallas import tpu as pltpu
from jax.sharding import PartitionSpec as P


NB, K, R, S = 8, 64, 64, 4
PARTS = 2
HALF = NB * K // PARTS
BF = jnp.bfloat16
F32 = jnp.float32


def pack_table():
    table = np.zeros((NB, 2, 16), np.int32)
    for t in range(NB):
        pairs = [(j, i) for j in range(t + 1) for i in range(t + 1, NB)]
        for s, (j, i) in enumerate(pairs):
            table[t, :, s] = (j, i)
    return table


def shift(axis_size, by):
    return [(i, (i + by) % axis_size) for i in range(axis_size)]


def pick(arrays, index):
    out = arrays[-1]
    for n in range(len(arrays) - 2, -1, -1):
        out = jnp.where(index == n, arrays[n], out)
    return out


def nt_dot(a, b):
    return lax.dot_general(a, b, (((1,), (1,)), ((), ())), preferred_element_type=F32)


def row_copies(meta, pieces, a_ref, sems):
    copies = []
    for s, piece in enumerate(pieces):
        source = (meta[33] + (S - s)) % S
        for b in range(NB // PARTS):
            rows = pl.ds(pl.multiple_of(b * K + source * 16, 16), 16)
            copies.append(pltpu.make_async_copy(piece.at[b], a_ref.at[rows], sems.at[s, b]))
    return copies


def old_send_kernel(guess_ref, r_ref, out_ref):
    product = nt_dot(guess_ref[...].astype(BF), r_ref[...])
    left = lax.broadcasted_iota(jnp.int32, (8, 128), 1) < 64
    for m in range(NB // 2):
        upper = product[:8, m * 128 : (m + 1) * 128]
        lower = product[8:, m * 128 : (m + 1) * 128]
        even = jnp.where(left, upper, pltpu.roll(lower, 64, 1))
        odd = jnp.where(left, pltpu.roll(upper, 64, 1), lower)
        for d in range(S):
            out_ref[2 * m, d] = even
            out_ref[2 * m + 1, d] = odd


def old_sum_kernel(meta, ranks, in_ref, out_ref):
    t = meta[0]
    column = lax.broadcasted_iota(jnp.int32, (8, 128), 1) % K
    for j in range(NB):
        total = (in_ref[j, 0] + in_ref[j, 1]) + (in_ref[j, 2] + in_ref[j, 3])
        rank = jnp.where(t < j, ranks[t, j], 0)
        out_ref[j] = jnp.where(column < rank, total, 0.0).astype(BF)


def unpack_old(meta, packed, old_ref):
    left = lax.broadcasted_iota(jnp.int32, (8, 128), 1) < 64
    for s, packed_ref in enumerate(packed):
        source = (meta[33] + (S - s)) % S
        rows = pl.ds(pl.multiple_of(source * 16, 16), 16)
        for m in range(NB // 2):
            even = packed_ref[2 * m].astype(F32)
            odd = packed_ref[2 * m + 1].astype(F32)
            upper = jnp.where(left, even, pltpu.roll(odd, 64, 1))
            lower = jnp.where(left, pltpu.roll(even, 64, 1), odd)
            both = jnp.concatenate([upper, lower], axis=0).astype(BF)
            old_ref[rows, m * 128 : (m + 1) * 128] = both


def fetch_operands(inv_hbm, r_hbm, inv_v, r_v, sems):
    fetch = [
        pltpu.make_async_copy(inv_hbm.at[:, pl.ds(n * 512, 512)], inv_v.at[n], sems.at[n])
        for n in range(4)
    ]
    whole = pltpu.make_async_copy(r_hbm, r_v, sems.at[4])
    fetch[0].start()
    whole.start()
    for n in range(1, 4):
        fetch[n].start()
    return fetch, whole


def products(fetch, whole, a_ref, inv_v, r_v, x_ref, h_ref, base):
    for n in range(4):
        cols = pl.ds(n * 512, 512)
        fetch[n].wait()
        x = jnp.dot(a_ref[...], inv_v[n], preferred_element_type=F32)
        low = x.astype(BF)
        x_ref[:, cols] = low
        if n == 0:
            whole.wait()
        part = nt_dot(low, r_v[:, cols])
        for m in range(4):
            piece = part[:, m * 128 : (m + 1) * 128]
            if n == 0:
                h_ref[m, base : base + HALF] = piece
            else:
                h_ref[m, base : base + HALF] += piece


def first_kernel(
    meta, p0, p1, p2, p3, inv_hbm, r_hbm, x_ref, h_ref, a_ref, inv_v, r_v, row_sems, sems
):
    rows = row_copies(meta, (p0, p1, p2, p3), a_ref, row_sems)
    for copy in rows:
        copy.start()
    fetch, whole = fetch_operands(inv_hbm, r_hbm, inv_v, r_v, sems)
    for copy in rows:
        copy.wait()
    products(fetch, whole, a_ref, inv_v, r_v, x_ref, h_ref, 0)


def second_kernel(
    meta, p0, p1, p2, p3, inv_hbm, r_hbm, o0, o1, o2, o3, h0_ref,
    x_ref, pack_ref, old_ref, h_s, a_ref, inv_v, r_v, row_sems, sems,
):
    rows = row_copies(meta, (p0, p1, p2, p3), a_ref, row_sems)
    for copy in rows:
        copy.start()
    fetch, whole = fetch_operands(inv_hbm, r_hbm, inv_v, r_v, sems)
    unpack_old(meta, (o0, o1, o2, o3), old_ref)
    for m in range(4):
        h_s[m, :HALF] = h0_ref[m]
    for copy in rows:
        copy.wait()
    products(fetch, whole, a_ref, inv_v, r_v, x_ref, h_s, HALF)
    own = pl.ds(pl.multiple_of(meta[0] * K, K), K)
    for m in range(4):
        fold = jnp.dot(old_ref[...], h_s[m].astype(BF), preferred_element_type=F32)
        h_s[m, own, :] = h_s[m, own, :] - fold
    lane = lax.broadcasted_iota(jnp.int32, (32, 128), 1)
    for s in range(16):
        j = meta[1 + s]
        i = meta[17 + s]
        block = h_s[i // 2, pl.ds(pl.multiple_of(j * K, K), K), :]
        swapped = pltpu.roll(block, 64, 1)
        odd = (i % 2) == 1
        even_lanes = jnp.where(odd, swapped, block)
        odd_lanes = jnp.where(odd, block, swapped)
        pack_ref[s] = jnp.where(lane < 64, even_lanes[:32], odd_lanes[32:]).astype(BF)


def chain_kernel(meta, ranks, hg_ref, old_ref, x0_ref, x1_ref, out_ref, c_s):
    def block(t, s):
        packed = hg_ref[t, s]
        return jnp.concatenate([packed[:, :64], packed[:, 64:]], axis=0)

    coef = {}
    lane = lax.broadcasted_iota(jnp.int32, (R, K), 1)
    c_s[0] = jnp.zeros((R, NB * K), BF)
    for t in range(NB):
        count = NB - 1 - t
        if t > 0:
            incoming = [coef[j, t] for j in range(t)]
            filler = [jnp.zeros((R, K), BF)] * (NB - t)
            c_s[t] = jnp.concatenate(incoming + filler, axis=1)
        if count == 0:
            break
        y = jnp.concatenate([block(t, t * count + b) for b in range(count)], axis=1).astype(F32)
        if t > 0:
            g = jnp.concatenate(
                [
                    jnp.concatenate([block(t, a * count + b) for b in range(count)], axis=1)
                    for a in range(t)
                ],
                axis=0,
            )
            y = y - jnp.dot(jnp.concatenate(incoming, axis=1), g, preferred_element_type=F32)
        for b in range(count):
            i = t + 1 + b
            piece = y[:, b * K : (b + 1) * K]
            coef[t, i] = jnp.where(lane < ranks[i, t], piece, 0.0).astype(BF)
    mine = meta[0]
    total = c_s[mine] + old_ref[...]
    own = pl.ds(pl.multiple_of((mine % 4) * K, K), K)
    own_rows = jnp.where(mine < 4, x0_ref[own, :], x1_ref[own, :])
    sums = jnp.dot(total[:, :HALF], x0_ref[...], preferred_element_type=F32)
    sums = sums + jnp.dot(total[:, HALF:], x1_ref[...], preferred_element_type=F32)
    out_ref[...] = own_rows.astype(F32) - sums


def program(right_side, guess, inverse, left_factor, right_factor, ranks):
    t = lax.axis_index("row")
    q = lax.axis_index("col")
    p = lax.axis_index("rhs")
    left = left_factor[0]
    right = right_factor[0].reshape(NB * K, -1)
    m = left.shape[2]

    per = NB // PARTS
    own_rows = right_side[0].astype(BF)[None]
    parts = []
    for n in range(PARTS):
        part = lax.dynamic_slice(left, (n * per, 16 * p, 0), (per, 16, m))
        own_block = lax.broadcasted_iota(jnp.int32, (per, 1, 1), 0) + n * per == t
        parts.append(jnp.where(own_block, own_rows, part))
    parts = lax.optimization_barrier(tuple(parts))
    halves = []
    for n in range(PARTS):
        part = parts[n]
        over_col = [part] + [lax.ppermute(part, "col", shift(S, d)) for d in range(1, S)]
        over_rhs = []
        for s in range(S):
            piece = pick(over_col, (q - p - s) % S)
            over_rhs.append(piece if s == 0 else lax.ppermute(piece, "rhs", shift(S, s)))
        halves.append(over_rhs)

    table = jnp.asarray(pack_table())
    mine = lax.dynamic_index_in_dim(table, t, 0, keepdims=False)
    meta = jnp.concatenate([t[None], mine.reshape(-1), p[None]]).astype(jnp.int32)
    vmem = pl.BlockSpec(memory_space=pltpu.VMEM)
    smem = pl.BlockSpec(memory_space=pltpu.SMEM)
    sends = pl.pallas_call(
        old_send_kernel,
        in_specs=[vmem, vmem],
        out_specs=vmem,
        out_shape=jax.ShapeDtypeStruct((NB, S, 8, 128), F32),
        compiler_params=pltpu.CompilerParams(vmem_limit_bytes=8 * 2**20),
        name="old_send",
    )(guess[0], right)
    arrived = lax.all_to_all(sends.reshape(NB * S, 8, 128), ("row", "col"), 0, 0, tiled=True)
    arrived = arrived.reshape(NB, S, 8, 128)
    own_old = pl.pallas_call(
        old_sum_kernel,
        in_specs=[smem, smem, vmem],
        out_specs=vmem,
        out_shape=jax.ShapeDtypeStruct((NB, 8, 128), BF),
        compiler_params=pltpu.CompilerParams(vmem_limit_bytes=8 * 2**20),
        name="old_sum",
    )(meta, ranks, arrived)
    packed_old = [own_old] + [lax.ppermute(own_old, "rhs", shift(S, s)) for s in range(1, S)]

    hbm = pl.BlockSpec(memory_space=pltpu.HBM)
    working = [
        pltpu.VMEM((HALF, m), BF),
        pltpu.VMEM((4, m, 512), BF),
        pltpu.VMEM((NB * K, m), BF),
        pltpu.SemaphoreType.DMA((S, NB // PARTS)),
        pltpu.SemaphoreType.DMA((5,)),
    ]
    x0, h0 = pl.pallas_call(
        first_kernel,
        in_specs=[smem] + [hbm] * 6,
        out_specs=[vmem] * 2,
        out_shape=[
            jax.ShapeDtypeStruct((HALF, m), BF),
            jax.ShapeDtypeStruct((4, HALF, 128), F32),
        ],
        scratch_shapes=working,
        compiler_params=pltpu.CompilerParams(vmem_limit_bytes=53 * 2**20),
        name="first",
    )(meta, *halves[0], inverse[0], right)
    x1, packed, old = pl.pallas_call(
        second_kernel,
        in_specs=[smem] + [hbm] * 6 + [vmem] * 5,
        out_specs=[vmem] * 3,
        out_shape=[
            jax.ShapeDtypeStruct((HALF, m), BF),
            jax.ShapeDtypeStruct((16, 32, 128), BF),
            jax.ShapeDtypeStruct((R, NB * K), BF),
        ],
        scratch_shapes=[pltpu.VMEM((4, NB * K, 128), F32)] + working,
        compiler_params=pltpu.CompilerParams(vmem_limit_bytes=53 * 2**20),
        name="second",
    )(meta, *halves[1], inverse[0], right, *packed_old, h0)

    summed = lax.all_to_all(packed, ("col", "rhs"), 0, 0, tiled=True)
    summed = summed.astype(F32).sum(axis=0).astype(BF)
    shared = lax.all_to_all(
        jnp.broadcast_to(summed[None], (128, 32, 128)), ("row", "col", "rhs"), 0, 0, tiled=True
    ).reshape(NB, 16, 32, 128)

    partial_solution = pl.pallas_call(
        chain_kernel,
        in_specs=[smem, smem, vmem, vmem, vmem, vmem],
        out_specs=vmem,
        out_shape=jax.ShapeDtypeStruct((R, m), F32),
        scratch_shapes=[pltpu.VMEM((NB, R, NB * K), BF)],
        compiler_params=pltpu.CompilerParams(vmem_limit_bytes=16 * 2**20),
        name="sweep",
    )(meta, ranks, shared, old, x0, x1)

    result = lax.dynamic_slice(partial_solution, (16 * p, 0), (16, m))
    for s in range(1, S):
        send = lax.dynamic_slice(partial_solution, (16 * ((p + s) % S), 0), (16, m)).astype(BF)
        result = result + lax.ppermute(send, "rhs", shift(S, s)).astype(F32)
    return result[None]


def solution(mesh):
    in_specs = (
        P("row", "rhs", "col"),
        P("row", "rhs", "col"),
        P("row", "rhs", "col"),
        P("row", None, None, "col"),
        P("row", None, None, "col"),
        P(),
    )
    out_specs = P("row", "rhs", "col")
    return jax.shard_map(program, mesh=mesh, in_specs=in_specs, out_specs=out_specs, check_vma=False)
```

profile of v0, /device:TPU:0, one launch (start us, length us, event | category | flops | bytes accessed | tf_op | source)
XLA Modules:
  0.0 126.6 jit_solution(8980715498487130477)
XLA Ops:
  2.1 3.4 %collective-permute-start.10 = (bf16[4,16,2048]{2,1,0:T(8,128)(2,1)S(1)}, bf16[4,16,2048]{2,1,0:T(8,128)(2,1)S(1)}, u32[]{:S(2)}, u32[]{:S(2)}) collective-permute-start(bf16[4,16,2048]{2,1,0:T(8,128)(2,1)S(1)} %get-tuple-element.13), channel_id=1, source_target_pairs={{0,8},{4,12},{8,0},{12,4},{1,9},{5,13},{9,1},{13,5},{2,10},{6,14},... | collective-permute-start | bytes 786440 | tf_op jit(solution)/shard_map/ppermute | solution.py:219
  8.2 3.1 %collective-permute-start.1 = (bf16[4,16,2048]{2,1,0:T(8,128)(2,1)S(1)}, bf16[4,16,2048]{2,1,0:T(8,128)(2,1)S(1)}, u32[]{:S(2)}, u32[]{:S(2)}) collective-permute-start(bf16[4,16,2048]{2,1,0:T(8,128)(2,1)S(1)} %get-tuple-element.12), channel_id=1, source_target_pairs={{0,8},{4,12},{8,0},{12,4},{1,9},{5,13},{9,1},{13,5},{2,10},{6,14},... | collective-permute-start | bytes 786440 | tf_op jit(solution)/shard_map/ppermute | solution.py:219
  11.3 1.6 %copy-done = bf16[1,8,64,2048]{3,2,1,0:T(8,128)(2,1)S(1)} copy-done((bf16[1,8,64,2048]{3,2,1,0:T(8,128)(2,1)S(1)}, bf16[1,8,64,2048]{3,2,1,0:T(8,128)(2,1)}, u32[]{:S(2)}) %copy-start) | copy-done | bytes 2097176
  13.8 1.4 %old_send.1 = f32[8,4,8,128]{3,2,1,0:T(8,128)} custom-call(f32[16,2048]{1,0:T(8,128)S(1)} %bitcast.21, bf16[512,2048]{1,0:T(8,128)(2,1)S(1)} %bitcast.18), custom_call_target="tpu_custom_call" | custom-call | tf_op jit(solution)/shard_map/old_send/pallas_call | solution.py:231
  15.2 5.7 %all-to-all-start = ((f32[32,8,128]{2,1,0:T(8,128)}), f32[32,8,128]{2,1,0:T(8,128)S(1)}, u32[]{:S(2)}, u32[]{:S(2)}) async-start(f32[32,8,128]{2,1,0:T(8,128)} %bitcast.8), calls=%async_computation | async-start | bytes 262144 | tf_op jit(solution)/shard_map/all_to_all | solution.py:239
  21.7 11.7 %all-to-all-done = f32[32,8,128]{2,1,0:T(8,128)S(1)} async-done(((f32[32,8,128]{2,1,0:T(8,128)}), f32[32,8,128]{2,1,0:T(8,128)S(1)}, u32[]{:S(2)}, u32[]{:S(2)}) %all-to-all-start) | async-done | bytes 131104 | tf_op jit(solution)/shard_map/all_to_all | solution.py:239
  34.4 1.5 %collective-permute-start.6 = (bf16[8,8,128]{2,1,0:T(8,128)(2,1)S(1)}, bf16[8,8,128]{2,1,0:T(8,128)(2,1)S(1)}, u32[]{:S(2)}, u32[]{:S(2)}) collective-permute-start(bf16[8,8,128]{2,1,0:T(8,128)(2,1)S(1)} %old_sum.1.o0), channel_id=1, source_target_pairs={{0,1},{1,2},{2,3},{3,0},{4,5},{5,6},{6,7},{7,4},{8,9},{9,10},{10,1... | collective-permute-start | bytes 49160 | tf_op jit(solution)/shard_map/ppermute | solution.py:249
  36.1 1.6 %collective-permute-start.12 = (bf16[4,16,2048]{2,1,0:T(8,128)(2,1)S(1)}, bf16[4,16,2048]{2,1,0:T(8,128)(2,1)S(1)}, u32[]{:S(2)}, u32[]{:S(2)}) collective-permute-start(bf16[4,16,2048]{2,1,0:T(8,128)(2,1)S(1)} %get-tuple-element.23), channel_id=1, source_target_pairs={{0,1},{1,2},{2,3},{3,0},{4,5},{5,6},{6,7},{7,4},{8,9},{9,10},{10,1... | collective-permute-start | bytes 786440 | tf_op jit(solution)/shard_map/ppermute | solution.py:223
  37.6 1.7 %collective-permute-start.13 = (bf16[4,16,2048]{2,1,0:T(8,128)(2,1)S(1)}, bf16[4,16,2048]{2,1,0:T(8,128)(2,1)S(1)}, u32[]{:S(2)}, u32[]{:S(2)}) collective-permute-start(bf16[4,16,2048]{2,1,0:T(8,128)(2,1)S(1)} %get-tuple-element.22), channel_id=1, source_target_pairs={{0,2},{1,3},{2,0},{3,1},{4,6},{5,7},{6,4},{7,5},{8,10},{9,11},{10,... | collective-permute-start | bytes 786440 | tf_op jit(solution)/shard_map/ppermute | solution.py:223
  39.4 2.2 %collective-permute-start.14 = (bf16[4,16,2048]{2,1,0:T(8,128)(2,1)S(1)}, bf16[4,16,2048]{2,1,0:T(8,128)(2,1)S(1)}, u32[]{:S(2)}, u32[]{:S(2)}) collective-permute-start(bf16[4,16,2048]{2,1,0:T(8,128)(2,1)S(1)} %get-tuple-element.21), channel_id=1, source_target_pairs={{0,3},{1,0},{2,1},{3,2},{4,7},{5,4},{6,5},{7,6},{8,11},{9,8},{10,9... | collective-permute-start | bytes 786440 | tf_op jit(solution)/shard_map/ppermute | solution.py:223
  42.5 1.6 %collective-permute-start.3 = (bf16[4,16,2048]{2,1,0:T(8,128)(2,1)S(1)}, bf16[4,16,2048]{2,1,0:T(8,128)(2,1)S(1)}, u32[]{:S(2)}, u32[]{:S(2)}) collective-permute-start(bf16[4,16,2048]{2,1,0:T(8,128)(2,1)S(1)} %get-tuple-element.27), channel_id=1, source_target_pairs={{0,1},{1,2},{2,3},{3,0},{4,5},{5,6},{6,7},{7,4},{8,9},{9,10},{10,1... | collective-permute-start | bytes 786440 | tf_op jit(solution)/shard_map/ppermute | solution.py:223
  44.0 2.7 %collective-permute-start.4 = (bf16[4,16,2048]{2,1,0:T(8,128)(2,1)S(1)}, bf16[4,16,2048]{2,1,0:T(8,128)(2,1)S(1)}, u32[]{:S(2)}, u32[]{:S(2)}) collective-permute-start(bf16[4,16,2048]{2,1,0:T(8,128)(2,1)S(1)} %get-tuple-element.26), channel_id=1, source_target_pairs={{0,2},{1,3},{2,0},{3,1},{4,6},{5,7},{6,4},{7,5},{8,10},{9,11},{10,... | collective-permute-start | bytes 786440 | tf_op jit(solution)/shard_map/ppermute | solution.py:223
  46.8 3.4 %collective-permute-done.12.p1 = bf16[4,16,2048]{2,1,0:T(8,128)(2,1)S(1)} collective-permute-done((bf16[4,16,2048]{2,1,0:T(8,128)(2,1)S(1)}, bf16[4,16,2048]{2,1,0:T(8,128)(2,1)S(1)}, u32[]{:S(2)}, u32[]{:S(2)}) %collective-permute-start.12) | collective-permute-done | bytes 262176 | tf_op jit(solution)/shard_map/ppermute | solution.py:223
  50.2 2.0 %collective-permute-done.13.p2 = bf16[4,16,2048]{2,1,0:T(8,128)(2,1)S(1)} collective-permute-done((bf16[4,16,2048]{2,1,0:T(8,128)(2,1)S(1)}, bf16[4,16,2048]{2,1,0:T(8,128)(2,1)S(1)}, u32[]{:S(2)}, u32[]{:S(2)}) %collective-permute-start.13) | collective-permute-done | bytes 262176 | tf_op jit(solution)/shard_map/ppermute | solution.py:223
  52.2 1.8 %collective-permute-start.7 = (bf16[8,8,128]{2,1,0:T(8,128)(2,1)S(1)}, bf16[8,8,128]{2,1,0:T(8,128)(2,1)S(1)}, u32[]{:S(2)}, u32[]{:S(2)}) collective-permute-start(bf16[8,8,128]{2,1,0:T(8,128)(2,1)S(1)} %old_sum.1.o0), channel_id=1, source_target_pairs={{0,2},{1,3},{2,0},{3,1},{4,6},{5,7},{6,4},{7,5},{8,10},{9,11},{10,... | collective-permute-start | bytes 49160 | tf_op jit(solution)/shard_map/ppermute | solution.py:249
  54.0 1.8 %collective-permute-start.8 = (bf16[8,8,128]{2,1,0:T(8,128)(2,1)S(1)}, bf16[8,8,128]{2,1,0:T(8,128)(2,1)S(1)}, u32[]{:S(2)}, u32[]{:S(2)}) collective-permute-start(bf16[8,8,128]{2,1,0:T(8,128)(2,1)S(1)} %old_sum.1.o0), channel_id=1, source_target_pairs={{0,3},{1,0},{2,1},{3,2},{4,7},{5,4},{6,5},{7,6},{8,11},{9,8},{10,9... | collective-permute-start | bytes 49160 | tf_op jit(solution)/shard_map/ppermute | solution.py:249
  55.8 9.6 %first.1 = (bf16[256,2048]{1,0:T(8,128)(2,1)}, f32[4,256,128]{2,1,0:T(8,128)}) custom-call(s32[34]{0:T(128)S(1)} %pad_add_fusion.meta, bf16[4,16,2048]{2,1,0:T(8,128)(2,1)S(1)} %get-tuple-element.24.p0, bf16[4,16,2048]{2,1,0:T(8,128)(2,1)S(1)} %collective-permute-done.12.p1, bf16[4,16,2048]{2,1,0:T(8,128)(2,1)S(1)} %collective-permute-done.13.p2, ...), custom_call_target="tpu_custom_call" | custom-call | tf_op jit(solution)/shard_map/first/pallas_call | solution.py:259
  66.2 10.6 %second.1 = (bf16[256,2048]{1,0:T(8,128)(2,1)}, bf16[16,32,128]{2,1,0:T(8,128)(2,1)S(1)}, bf16[64,512]{1,0:T(8,128)(2,1)S(1)}) custom-call(s32[34]{0:T(128)S(1)} %pad_add_fusion.meta, bf16[4,16,2048]{2,1,0:T(8,128)(2,1)S(1)} %get-tuple-element.28.p0, bf16[4,16,2048]{2,1,0:T(8,128)(2,1)S(1)} %collective-permute-done.3.p1, bf16[4,16,2048]{2,1,0:T(8,128)(2,1)} %copy-done.6, ...), custom_call_target="tpu_custom_call" | custom-call | tf_op jit(solution)/shard_map/second/pallas_call | solution.py:271
  76.8 13.7 %all_to_all.15 = bf16[16,32,128]{2,1,0:T(8,128)(2,1)S(1)} all-to-all(bf16[16,32,128]{2,1,0:T(8,128)(2,1)S(1)} %get-tuple-element.15), channel_id=1, replica_groups=mesh['row'=8,'col'=4,'rhs'=4] {'col','rhs'}, dimensions={0} | all-to-all | bytes 262144 | tf_op jit(solution)/shard_map/all_to_all | solution.py:285
  91.7 5.8 %all-to-all-start.2 = ((bf16[128,32,128]{2,1,0:T(8,128)(2,1)}), bf16[128,32,128]{2,1,0:T(8,128)(2,1)S(1)}, u32[]{:S(2)}, u32[]{:S(2)}) async-start(bf16[128,32,128]{2,1,0:T(8,128)(2,1)} %broadcast_in_dim.48), calls=%async_computation.2 | async-start | bytes 2097152 | tf_op jit(solution)/shard_map/all_to_all | solution.py:287
  97.6 19.0 %all-to-all-done.2 = bf16[128,32,128]{2,1,0:T(8,128)(2,1)S(1)} async-done(((bf16[128,32,128]{2,1,0:T(8,128)(2,1)}), bf16[128,32,128]{2,1,0:T(8,128)(2,1)S(1)}, u32[]{:S(2)}, u32[]{:S(2)}) %all-to-all-start.2) | async-done | bytes 1048608 | tf_op jit(solution)/shard_map/all_to_all | solution.py:287
  116.6 2.1 %sweep.1 = f32[64,2048]{1,0:T(8,128)S(1)} custom-call(s32[34]{0:T(128)S(1)} %pad_add_fusion.meta, s32[8,8]{1,0:T(8,128)S(1)} %copy-done.4, bf16[8,16,32,128]{3,2,1,0:T(8,128)(2,1)S(1)} %bitcast.19, bf16[64,512]{1,0:T(8,128)(2,1)S(1)} %get-tuple-element.16.old_ref, bf16[256,2048]{1,0:T(8,128)(2,1)S(1)} %copy-done.1, bf16[256,2048]{1,0:T(8,128)(2,1)S(1)} %copy-done.2), custom_call_target="tpu_custom_call" | custom-call | tf_op jit(solution)/shard_map/sweep/pallas_call | solution.py:291
  119.5 1.8 %collective-permute-start.16 = (bf16[16,2048]{1,0:T(8,128)(2,1)S(1)}, bf16[16,2048]{1,0:T(8,128)(2,1)S(1)}, u32[]{:S(2)}, u32[]{:S(2)}) collective-permute-start(bf16[16,2048]{1,0:T(8,128)(2,1)S(1)} %get-tuple-element.31), channel_id=1, source_target_pairs={{0,2},{1,3},{2,0},{3,1},{4,6},{5,7},{6,4},{7,5},{8,10},{9,11},{10,... | collective-permute-start | bytes 196616 | tf_op jit(solution)/shard_map/ppermute | solution.py:304
  122.3 3.1 %collective-permute-done.15 = bf16[16,2048]{1,0:T(8,128)(2,1)S(1)} collective-permute-done((bf16[16,2048]{1,0:T(8,128)(2,1)S(1)}, bf16[16,2048]{1,0:T(8,128)(2,1)S(1)}, u32[]{:S(2)}, u32[]{:S(2)}) %collective-permute-start.15) | collective-permute-done | bytes 65568 | tf_op jit(solution)/shard_map/ppermute | solution.py:304
  (50 shorter events, 13.6 us)
Async XLA Ops:
  0.0 33.4 %copy-start.4 = (s32[8,8]{1,0:T(8,128)S(1)}, s32[8,8]{1,0:T(8,128)}, u32[]{:S(2)}) copy-start(s32[8,8]{1,0:T(8,128)} %ranks.3) | copy-start | bytes 772
  2.1 31.9 %collective-permute-start.10 = (bf16[4,16,2048]{2,1,0:T(8,128)(2,1)S(1)}, bf16[4,16,2048]{2,1,0:T(8,128)(2,1)S(1)}, u32[]{:S(2)}, u32[]{:S(2)}) collective-permute-start(bf16[4,16,2048]{2,1,0:T(8,128)(2,1)S(1)} %get-tuple-element.13), channel_id=1, source_target_pairs={{0,8},{4,12},{8,0},{12,4},{1,9},{5,13},{9,1},{13,5},{2,10},{6,14},... | collective-permute-start | bytes 786440 | tf_op jit(solution)/shard_map/ppermute | solution.py:219
  5.5 28.9 %collective-permute-start.11 = (bf16[4,16,2048]{2,1,0:T(8,128)(2,1)S(1)}, bf16[4,16,2048]{2,1,0:T(8,128)(2,1)S(1)}, u32[]{:S(2)}, u32[]{:S(2)}) collective-permute-start(bf16[4,16,2048]{2,1,0:T(8,128)(2,1)S(1)} %get-tuple-element.13), channel_id=1, source_target_pairs={{0,12},{4,0},{8,4},{12,8},{1,13},{5,1},{9,5},{13,9},{2,14},{6,2},{... | collective-permute-start | bytes 786440 | tf_op jit(solution)/shard_map/ppermute | solution.py:219
  6.6 29.4 %collective-permute-start.9 = (bf16[4,16,2048]{2,1,0:T(8,128)(2,1)S(1)}, bf16[4,16,2048]{2,1,0:T(8,128)(2,1)S(1)}, u32[]{:S(2)}, u32[]{:S(2)}) collective-permute-start(bf16[4,16,2048]{2,1,0:T(8,128)(2,1)S(1)} %get-tuple-element.13), channel_id=1, source_target_pairs={{0,4},{4,8},{8,12},{12,0},{1,5},{5,9},{9,13},{13,1},{2,6},{6,10},{... | collective-permute-start | bytes 786440 | tf_op jit(solution)/shard_map/ppermute | solution.py:219
  7.5 30.1 %collective-permute-start = (bf16[4,16,2048]{2,1,0:T(8,128)(2,1)S(1)}, bf16[4,16,2048]{2,1,0:T(8,128)(2,1)S(1)}, u32[]{:S(2)}, u32[]{:S(2)}) collective-permute-start(bf16[4,16,2048]{2,1,0:T(8,128)(2,1)S(1)} %get-tuple-element.12), channel_id=1, source_target_pairs={{0,4},{4,8},{8,12},{12,0},{1,5},{5,9},{9,13},{13,1},{2,6},{6,10},{... | collective-permute-start | bytes 786440 | tf_op jit(solution)/shard_map/ppermute | solution.py:219
  8.2 31.1 %collective-permute-start.1 = (bf16[4,16,2048]{2,1,0:T(8,128)(2,1)S(1)}, bf16[4,16,2048]{2,1,0:T(8,128)(2,1)S(1)}, u32[]{:S(2)}, u32[]{:S(2)}) collective-permute-start(bf16[4,16,2048]{2,1,0:T(8,128)(2,1)S(1)} %get-tuple-element.12), channel_id=1, source_target_pairs={{0,8},{4,12},{8,0},{12,4},{1,9},{5,13},{9,1},{13,5},{2,10},{6,14},... | collective-permute-start | bytes 786440 | tf_op jit(solution)/shard_map/ppermute | solution.py:219
  15.2 18.2 %all-to-all-start = ((f32[32,8,128]{2,1,0:T(8,128)}), f32[32,8,128]{2,1,0:T(8,128)S(1)}, u32[]{:S(2)}, u32[]{:S(2)}) async-start(f32[32,8,128]{2,1,0:T(8,128)} %bitcast.8), calls=%async_computation | async-start | bytes 262144 | tf_op jit(solution)/shard_map/all_to_all | solution.py:239
  34.0 8.3 %collective-permute-start.2 = (bf16[4,16,2048]{2,1,0:T(8,128)(2,1)S(1)}, bf16[4,16,2048]{2,1,0:T(8,128)(2,1)S(1)}, u32[]{:S(2)}, u32[]{:S(2)}) collective-permute-start(bf16[4,16,2048]{2,1,0:T(8,128)(2,1)S(1)} %get-tuple-element.12), channel_id=1, source_target_pairs={{0,12},{4,0},{8,4},{12,8},{1,13},{5,1},{9,5},{13,9},{2,14},{6,2},{... | collective-permute-start | bytes 786440 | tf_op jit(solution)/shard_map/ppermute | solution.py:219
  34.4 9.6 %collective-permute-start.6 = (bf16[8,8,128]{2,1,0:T(8,128)(2,1)S(1)}, bf16[8,8,128]{2,1,0:T(8,128)(2,1)S(1)}, u32[]{:S(2)}, u32[]{:S(2)}) collective-permute-start(bf16[8,8,128]{2,1,0:T(8,128)(2,1)S(1)} %old_sum.1.o0), channel_id=1, source_target_pairs={{0,1},{1,2},{2,3},{3,0},{4,5},{5,6},{6,7},{7,4},{8,9},{9,10},{10,1... | collective-permute-start | bytes 49160 | tf_op jit(solution)/shard_map/ppermute | solution.py:249
  36.1 14.1 %collective-permute-start.12 = (bf16[4,16,2048]{2,1,0:T(8,128)(2,1)S(1)}, bf16[4,16,2048]{2,1,0:T(8,128)(2,1)S(1)}, u32[]{:S(2)}, u32[]{:S(2)}) collective-permute-start(bf16[4,16,2048]{2,1,0:T(8,128)(2,1)S(1)} %get-tuple-element.23), channel_id=1, source_target_pairs={{0,1},{1,2},{2,3},{3,0},{4,5},{5,6},{6,7},{7,4},{8,9},{9,10},{10,1... | collective-permute-start | bytes 786440 | tf_op jit(solution)/shard_map/ppermute | solution.py:223
  37.6 14.5 %collective-permute-start.13 = (bf16[4,16,2048]{2,1,0:T(8,128)(2,1)S(1)}, bf16[4,16,2048]{2,1,0:T(8,128)(2,1)S(1)}, u32[]{:S(2)}, u32[]{:S(2)}) collective-permute-start(bf16[4,16,2048]{2,1,0:T(8,128)(2,1)S(1)} %get-tuple-element.22), channel_id=1, source_target_pairs={{0,2},{1,3},{2,0},{3,1},{4,6},{5,7},{6,4},{7,5},{8,10},{9,11},{10,... | collective-permute-start | bytes 786440 | tf_op jit(solution)/shard_map/ppermute | solution.py:223
  39.4 14.6 %collective-permute-start.14 = (bf16[4,16,2048]{2,1,0:T(8,128)(2,1)S(1)}, bf16[4,16,2048]{2,1,0:T(8,128)(2,1)S(1)}, u32[]{:S(2)}, u32[]{:S(2)}) collective-permute-start(bf16[4,16,2048]{2,1,0:T(8,128)(2,1)S(1)} %get-tuple-element.21), channel_id=1, source_target_pairs={{0,3},{1,0},{2,1},{3,2},{4,7},{5,4},{6,5},{7,6},{8,11},{9,8},{10,9... | collective-permute-start | bytes 786440 | tf_op jit(solution)/shard_map/ppermute | solution.py:223
  42.5 23.0 %collective-permute-start.3 = (bf16[4,16,2048]{2,1,0:T(8,128)(2,1)S(1)}, bf16[4,16,2048]{2,1,0:T(8,128)(2,1)S(1)}, u32[]{:S(2)}, u32[]{:S(2)}) collective-permute-start(bf16[4,16,2048]{2,1,0:T(8,128)(2,1)S(1)} %get-tuple-element.27), channel_id=1, source_target_pairs={{0,1},{1,2},{2,3},{3,0},{4,5},{5,6},{6,7},{7,4},{8,9},{9,10},{10,1... | collective-permute-start | bytes 786440 | tf_op jit(solution)/shard_map/ppermute | solution.py:223
  44.0 21.4 %collective-permute-start.4 = (bf16[4,16,2048]{2,1,0:T(8,128)(2,1)S(1)}, bf16[4,16,2048]{2,1,0:T(8,128)(2,1)S(1)}, u32[]{:S(2)}, u32[]{:S(2)}) collective-permute-start(bf16[4,16,2048]{2,1,0:T(8,128)(2,1)S(1)} %get-tuple-element.26), channel_id=1, source_target_pairs={{0,2},{1,3},{2,0},{3,1},{4,6},{5,7},{6,4},{7,5},{8,10},{9,11},{10,... | collective-permute-start | bytes 786440 | tf_op jit(solution)/shard_map/ppermute | solution.py:223
  50.2 15.3 %collective-permute-start.5 = (bf16[4,16,2048]{2,1,0:T(8,128)(2,1)S(1)}, bf16[4,16,2048]{2,1,0:T(8,128)(2,1)S(1)}, u32[]{:S(2)}, u32[]{:S(2)}) collective-permute-start(bf16[4,16,2048]{2,1,0:T(8,128)(2,1)S(1)} %get-tuple-element.25), channel_id=1, source_target_pairs={{0,3},{1,0},{2,1},{3,2},{4,7},{5,4},{6,5},{7,6},{8,11},{9,8},{10,9... | collective-permute-start | bytes 786440 | tf_op jit(solution)/shard_map/ppermute | solution.py:223
  52.2 13.3 %collective-permute-start.7 = (bf16[8,8,128]{2,1,0:T(8,128)(2,1)S(1)}, bf16[8,8,128]{2,1,0:T(8,128)(2,1)S(1)}, u32[]{:S(2)}, u32[]{:S(2)}) collective-permute-start(bf16[8,8,128]{2,1,0:T(8,128)(2,1)S(1)} %old_sum.1.o0), channel_id=1, source_target_pairs={{0,2},{1,3},{2,0},{3,1},{4,6},{5,7},{6,4},{7,5},{8,10},{9,11},{10,... | collective-permute-start | bytes 49160 | tf_op jit(solution)/shard_map/ppermute | solution.py:249
  54.0 1.8 %copy-start.5 = (bf16[4,16,2048]{2,1,0:T(8,128)(2,1)}, bf16[4,16,2048]{2,1,0:T(8,128)(2,1)S(1)}, u32[]{:S(2)}) copy-start(bf16[4,16,2048]{2,1,0:T(8,128)(2,1)S(1)} %collective-permute-done.14.p3) | copy-start | bytes 786436
  54.0 11.4 %collective-permute-start.8 = (bf16[8,8,128]{2,1,0:T(8,128)(2,1)S(1)}, bf16[8,8,128]{2,1,0:T(8,128)(2,1)S(1)}, u32[]{:S(2)}, u32[]{:S(2)}) collective-permute-start(bf16[8,8,128]{2,1,0:T(8,128)(2,1)S(1)} %old_sum.1.o0), channel_id=1, source_target_pairs={{0,3},{1,0},{2,1},{3,2},{4,7},{5,4},{6,5},{7,6},{8,11},{9,8},{10,9... | collective-permute-start | bytes 49160 | tf_op jit(solution)/shard_map/ppermute | solution.py:249
  76.8 39.8 %copy-start.1 = (bf16[256,2048]{1,0:T(8,128)(2,1)S(1)}, bf16[256,2048]{1,0:T(8,128)(2,1)}, u32[]{:S(2)}) copy-start(bf16[256,2048]{1,0:T(8,128)(2,1)} %get-tuple-element.17.x0_ref) | copy-start | bytes 3145732
  76.8 39.8 %copy-start.2 = (bf16[256,2048]{1,0:T(8,128)(2,1)S(1)}, bf16[256,2048]{1,0:T(8,128)(2,1)}, u32[]{:S(2)}) copy-start(bf16[256,2048]{1,0:T(8,128)(2,1)} %get-tuple-element.18.x1_ref) | copy-start | bytes 3145732
  91.7 24.9 %all-to-all-start.2 = ((bf16[128,32,128]{2,1,0:T(8,128)(2,1)}), bf16[128,32,128]{2,1,0:T(8,128)(2,1)S(1)}, u32[]{:S(2)}, u32[]{:S(2)}) async-start(bf16[128,32,128]{2,1,0:T(8,128)(2,1)} %broadcast_in_dim.48), calls=%async_computation.2 | async-start | bytes 2097152 | tf_op jit(solution)/shard_map/all_to_all | solution.py:287
  118.8 6.6 %collective-permute-start.15 = (bf16[16,2048]{1,0:T(8,128)(2,1)S(1)}, bf16[16,2048]{1,0:T(8,128)(2,1)S(1)}, u32[]{:S(2)}, u32[]{:S(2)}) collective-permute-start(bf16[16,2048]{1,0:T(8,128)(2,1)S(1)} %get-tuple-element.29), channel_id=1, source_target_pairs={{0,1},{1,2},{2,3},{3,0},{4,5},{5,6},{6,7},{7,4},{8,9},{9,10},{10,1... | collective-permute-start | bytes 196616 | tf_op jit(solution)/shard_map/ppermute | solution.py:304
  119.5 5.9 %collective-permute-start.16 = (bf16[16,2048]{1,0:T(8,128)(2,1)S(1)}, bf16[16,2048]{1,0:T(8,128)(2,1)S(1)}, u32[]{:S(2)}, u32[]{:S(2)}) collective-permute-start(bf16[16,2048]{1,0:T(8,128)(2,1)S(1)} %get-tuple-element.31), channel_id=1, source_target_pairs={{0,2},{1,3},{2,0},{3,1},{4,6},{5,7},{6,4},{7,5},{8,10},{9,11},{10,... | collective-permute-start | bytes 196616 | tf_op jit(solution)/shard_map/ppermute | solution.py:304
  121.3 4.6 %collective-permute-start.17 = (bf16[16,2048]{1,0:T(8,128)(2,1)S(1)}, bf16[16,2048]{1,0:T(8,128)(2,1)S(1)}, u32[]{:S(2)}, u32[]{:S(2)}) collective-permute-start(bf16[16,2048]{1,0:T(8,128)(2,1)S(1)} %get-tuple-element.30), channel_id=1, source_target_pairs={{0,3},{1,0},{2,1},{3,2},{4,7},{5,4},{6,5},{7,6},{8,11},{9,8},{10,9... | collective-permute-start | bytes 196616 | tf_op jit(solution)/shard_map/ppermute | solution.py:304
  (4 other events, 4.0 us)
where the time goes:
time: 127 us
  waiting for transfers between devices  40.5 us (32%)
  starting transfers between devices  39.4 us (31%)
  Pallas kernels  24.3 us (19%)
  blocking collectives  13.7 us (11%)
  local copies, waits for them, and re-layouts  5.22 us (4%)
  other arithmetic  3.16 us (2%)
    all_to_all x1, waiting for transfers between devices, program(): lax.all_to_all(jnp.broadcast_to(summed[None], (128, 32, 128)), ('row', 'c...  19 us
    all_to_all x1, blocking collectives, program(): summed = lax.all_to_all(packed, ('col', 'rhs'), 0, 0, tiled=True)  13.7 us
    all_to_all x1, waiting for transfers between devices, program(): lax.all_to_all(sends.reshape(NB * S, 8, 128), ('row', 'col'), 0, 0, tiled...  11.7 us
    pallas_call x1, Pallas kernels, program(): pl.pallas_call(second_kernel, in_specs=[smem] + [hbm] * 6 + [vmem] * 5, o...  10.6 us
    ppermute x6, starting transfers between devices, program(): lax.ppermute(piece, 'rhs', shift(S, s))  9.72 us
    pallas_call x1, Pallas kernels, program(): pl.pallas_call(first_kernel, in_specs=[smem] + [hbm] * 6, out_specs=[vmem...  9.61 us
    ppermute x6, starting transfers between devices, program(): lax.ppermute(part, 'col', shift(S, d))  9.55 us
    all_to_all x1, starting transfers between devices, program(): lax.all_to_all(jnp.broadcast_to(summed[None], (128, 32, 128)), ('row', 'c...  5.83 us
  transfers between devices with their start and end apart: 20, of which 7 were waited for; matrix products, arithmetic and copies ran while one was open for 1% of the time, Pallas kernels for 9%

commit v1 on v0

--- a/solution.py
+++ b/solution.py
@@ -37,16 +37,6 @@
 
 def nt_dot(a, b):
     return lax.dot_general(a, b, (((1,), (1,)), ((), ())), preferred_element_type=F32)
-
-
-def row_copies(meta, pieces, a_ref, sems):
-    copies = []
-    for s, piece in enumerate(pieces):
-        source = (meta[33] + (S - s)) % S
-        for b in range(NB // PARTS):
-            rows = pl.ds(pl.multiple_of(b * K + source * 16, 16), 16)
-            copies.append(pltpu.make_async_copy(piece.at[b], a_ref.at[rows], sems.at[s, b]))
-    return copies
 
 
 def old_send_kernel(guess_ref, r_ref, out_ref):
@@ -85,63 +75,23 @@
             old_ref[rows, m * 128 : (m + 1) * 128] = both
 
 
-def fetch_operands(inv_hbm, r_hbm, inv_v, r_v, sems):
-    fetch = [
-        pltpu.make_async_copy(inv_hbm.at[:, pl.ds(n * 512, 512)], inv_v.at[n], sems.at[n])
-        for n in range(4)
-    ]
-    whole = pltpu.make_async_copy(r_hbm, r_v, sems.at[4])
-    fetch[0].start()
-    whole.start()
-    for n in range(1, 4):
-        fetch[n].start()
-    return fetch, whole
-
-
-def products(fetch, whole, a_ref, inv_v, r_v, x_ref, h_ref, base):
-    for n in range(4):
-        cols = pl.ds(n * 512, 512)
-        fetch[n].wait()
-        x = jnp.dot(a_ref[...], inv_v[n], preferred_element_type=F32)
-        low = x.astype(BF)
-        x_ref[:, cols] = low
-        if n == 0:
-            whole.wait()
-        part = nt_dot(low, r_v[:, cols])
-        for m in range(4):
-            piece = part[:, m * 128 : (m + 1) * 128]
-            if n == 0:
-                h_ref[m, base : base + HALF] = piece
-            else:
-                h_ref[m, base : base + HALF] += piece
-
-
-def first_kernel(
-    meta, p0, p1, p2, p3, inv_hbm, r_hbm, x_ref, h_ref, a_ref, inv_v, r_v, row_sems, sems
+def first_kernel(a_ref, inv_ref, r_ref, x_ref, h_ref):
+    x_ref[...] = jnp.dot(a_ref[...], inv_ref[...], preferred_element_type=F32).astype(BF)
+    part = nt_dot(x_ref[...], r_ref[...])
+    for m in range(4):
+        h_ref[m] = part[:, m * 128 : (m + 1) * 128]
+
+
+def second_kernel(
+    meta, a_ref, inv_ref, r_ref, o0, o1, o2, o3, h0_ref, x_ref, pack_ref, old_ref, h_s
 ):
-    rows = row_copies(meta, (p0, p1, p2, p3), a_ref, row_sems)
-    for copy in rows:
-        copy.start()
-    fetch, whole = fetch_operands(inv_hbm, r_hbm, inv_v, r_v, sems)
-    for copy in rows:
-        copy.wait()
-    products(fetch, whole, a_ref, inv_v, r_v, x_ref, h_ref, 0)
-
-
-def second_kernel(
-    meta, p0, p1, p2, p3, inv_hbm, r_hbm, o0, o1, o2, o3, h0_ref,
-    x_ref, pack_ref, old_ref, h_s, a_ref, inv_v, r_v, row_sems, sems,
-):
-    rows = row_copies(meta, (p0, p1, p2, p3), a_ref, row_sems)
-    for copy in rows:
-        copy.start()
-    fetch, whole = fetch_operands(inv_hbm, r_hbm, inv_v, r_v, sems)
     unpack_old(meta, (o0, o1, o2, o3), old_ref)
     for m in range(4):
         h_s[m, :HALF] = h0_ref[m]
-    for copy in rows:
-        copy.wait()
-    products(fetch, whole, a_ref, inv_v, r_v, x_ref, h_s, HALF)
+    x_ref[...] = jnp.dot(a_ref[...], inv_ref[...], preferred_element_type=F32).astype(BF)
+    part = nt_dot(x_ref[...], r_ref[...])
+    for m in range(4):
+        h_s[m, HALF:] = part[:, m * 128 : (m + 1) * 128]
     own = pl.ds(pl.multiple_of(meta[0] * K, K), K)
     for m in range(4):
         fold = jnp.dot(old_ref[...], h_s[m].astype(BF), preferred_element_type=F32)
@@ -221,7 +171,8 @@
         for s in range(S):
             piece = pick(over_col, (q - p - s) % S)
             over_rhs.append(piece if s == 0 else lax.ppermute(piece, "rhs", shift(S, s)))
-        halves.append(over_rhs)
+        ordered = [pick(over_rhs, (p - x) % S) for x in range(S)]
+        halves.append(jnp.stack(ordered, axis=1).reshape(HALF, m))
 
     table = jnp.asarray(pack_table())
     mine = lax.dynamic_index_in_dim(table, t, 0, keepdims=False)
@@ -248,39 +199,30 @@
     )(meta, ranks, arrived)
     packed_old = [own_old] + [lax.ppermute(own_old, "rhs", shift(S, s)) for s in range(1, S)]
 
-    hbm = pl.BlockSpec(memory_space=pltpu.HBM)
-    working = [
-        pltpu.VMEM((HALF, m), BF),
-        pltpu.VMEM((4, m, 512), BF),
-        pltpu.VMEM((NB * K, m), BF),
-        pltpu.SemaphoreType.DMA((S, NB // PARTS)),
-        pltpu.SemaphoreType.DMA((5,)),
-    ]
     x0, h0 = pl.pallas_call(
         first_kernel,
-        in_specs=[smem] + [hbm] * 6,
+        in_specs=[vmem] * 3,
         out_specs=[vmem] * 2,
         out_shape=[
             jax.ShapeDtypeStruct((HALF, m), BF),
             jax.ShapeDtypeStruct((4, HALF, 128), F32),
         ],
-        scratch_shapes=working,
-        compiler_params=pltpu.CompilerParams(vmem_limit_bytes=53 * 2**20),
+        compiler_params=pltpu.CompilerParams(vmem_limit_bytes=20 * 2**20),
         name="first",
-    )(meta, *halves[0], inverse[0], right)
+    )(halves[0], inverse[0], right)
     x1, packed, old = pl.pallas_call(
         second_kernel,
-        in_specs=[smem] + [hbm] * 6 + [vmem] * 5,
+        in_specs=[smem] + [vmem] * 8,
         out_specs=[vmem] * 3,
         out_shape=[
             jax.ShapeDtypeStruct((HALF, m), BF),
             jax.ShapeDtypeStruct((16, 32, 128), BF),
             jax.ShapeDtypeStruct((R, NB * K), BF),
         ],
-        scratch_shapes=[pltpu.VMEM((4, NB * K, 128), F32)] + working,
-        compiler_params=pltpu.CompilerParams(vmem_limit_bytes=53 * 2**20),
+        scratch_shapes=[pltpu.VMEM((4, NB * K, 128), F32)],
+        compiler_params=pltpu.CompilerParams(vmem_limit_bytes=22 * 2**20),
         name="second",
-    )(meta, *halves[1], inverse[0], right, *packed_old, h0)
+    )(meta, halves[1], inverse[0], right, *packed_old, h0)
 
     summed = lax.all_to_all(packed, ("col", "rhs"), 0, 0, tiled=True)
     summed = summed.astype(F32).sum(axis=0).astype(BF)

time: 127 us -> 126 us (level)
  Pallas kernels: 24.3 us -> 11.2 us
  waiting for transfers between devices: 40.5 us -> 51.8 us
  starting transfers between devices: 39.4 us -> 36.8 us
  blocking collectives: 13.7 us -> 15.9 us
    pallas_call x2, Pallas kernels: 20.2 us -> 7.11 us  [the longest x1 4.21 us: program(): pl.pallas_call(second_kernel, in_specs=[smem] + [vmem] * 8, out_specs=[vm...]
    ppermute x6, waiting for transfers between devices: 5.39 us -> 16.9 us  [program(): lax.ppermute(piece, 'rhs', shift(S, s))]
    all_to_all x1, blocking collectives: 13.7 us -> 15.9 us  [program(): summed = lax.all_to_all(packed, ('col', 'rhs'), 0, 0, tiled=True)]
    unnamed x16 -> x12, local copies, waits for them, and re-layouts: 3.28 us -> 3.83 us
  transfers between devices with their start and end apart: 20 -> 20, of which waited for: 7 -> 10; matrix products, arithmetic and copies ran while one was open for 1% -> 1% of each run, Pallas kernels for 9% -> 4%
where the time goes in v1:
time: 126 us
  waiting for transfers between devices  51.8 us (41%)
  starting transfers between devices  36.8 us (29%)
  blocking collectives  15.9 us (13%)
  Pallas kernels  11.2 us (9%)
  local copies, waits for them, and re-layouts  5.83 us (5%)
  other arithmetic  3.8 us (3%)
    all_to_all x1, waiting for transfers between devices, program(): lax.all_to_all(jnp.broadcast_to(summed[None], (128, 32, 128)), ('row', 'c...  19 us
    ppermute x6, waiting for transfers between devices, program(): lax.ppermute(piece, 'rhs', shift(S, s))  16.9 us
    all_to_all x1, blocking collectives, program(): summed = lax.all_to_all(packed, ('col', 'rhs'), 0, 0, tiled=True)  15.9 us
    all_to_all x1, waiting for transfers between devices, program(): lax.all_to_all(sends.reshape(NB * S, 8, 128), ('row', 'col'), 0, 0, tiled...  11.7 us
    ppermute x6, starting transfers between devices, program(): lax.ppermute(part, 'col', shift(S, d))  9.56 us
    ppermute x6, starting transfers between devices, program(): lax.ppermute(piece, 'rhs', shift(S, s))  9.19 us
    all_to_all x1, starting transfers between devices, program(): lax.all_to_all(sends.reshape(NB * S, 8, 128), ('row', 'col'), 0, 0, tiled...  5.7 us
    all_to_all x1, starting transfers between devices, program(): lax.all_to_all(jnp.broadcast_to(summed[None], (128, 32, 128)), ('row', 'c...  4.63 us
  transfers between devices with their start and end apart: 20, of which 10 were waited for; matrix products, arithmetic and copies ran while one was open for 1% of the time, Pallas kernels for 4%

profile of v1, /device:TPU:0, one launch (start us, length us, event | category | flops | bytes accessed | tf_op | source)
XLA Modules:
  0.0 125.7 jit_solution(4550485825790095254)
XLA Ops:
  0.9 1.2 bitcast_select_fusion
  2.1 3.4 %collective-permute-start.10 = (bf16[4,16,2048]{2,1,0:T(8,128)(2,1)S(1)}, bf16[4,16,2048]{2,1,0:T(8,128)(2,1)S(1)}, u32[]{:S(2)}, u32[]{:S(2)}) collective-permute-start(bf16[4,16,2048]{2,1,0:T(8,128)(2,1)S(1)} %get-tuple-element.13), channel_id=1, source_target_pairs={{0,8},{4,12},{8,0},{12,4},{1,9},{5,13},{9,1},{13,5},{2,10},{6,14},... | collective-permute-start | bytes 786440 | tf_op jit(solution)/shard_map/ppermute | solution.py:169
  8.2 3.1 %collective-permute-start.1 = (bf16[4,16,2048]{2,1,0:T(8,128)(2,1)S(1)}, bf16[4,16,2048]{2,1,0:T(8,128)(2,1)S(1)}, u32[]{:S(2)}, u32[]{:S(2)}) collective-permute-start(bf16[4,16,2048]{2,1,0:T(8,128)(2,1)S(1)} %get-tuple-element.12), channel_id=1, source_target_pairs={{0,8},{4,12},{8,0},{12,4},{1,9},{5,13},{9,1},{13,5},{2,10},{6,14},... | collective-permute-start | bytes 786440 | tf_op jit(solution)/shard_map/ppermute | solution.py:169
  11.3 1.6 %copy-done = bf16[1,8,64,2048]{3,2,1,0:T(8,128)(2,1)S(1)} copy-done((bf16[1,8,64,2048]{3,2,1,0:T(8,128)(2,1)S(1)}, bf16[1,8,64,2048]{3,2,1,0:T(8,128)(2,1)}, u32[]{:S(2)}) %copy-start) | copy-done | bytes 2097176
  13.8 1.4 %old_send.1 = f32[8,4,8,128]{3,2,1,0:T(8,128)} custom-call(f32[16,2048]{1,0:T(8,128)S(1)} %bitcast.51, bf16[512,2048]{1,0:T(8,128)(2,1)S(1)} %bitcast.44), custom_call_target="tpu_custom_call" | custom-call | tf_op jit(solution)/shard_map/old_send/pallas_call | solution.py:182
  15.2 5.7 %all-to-all-start = ((f32[32,8,128]{2,1,0:T(8,128)}), f32[32,8,128]{2,1,0:T(8,128)S(1)}, u32[]{:S(2)}, u32[]{:S(2)}) async-start(f32[32,8,128]{2,1,0:T(8,128)} %bitcast.16), calls=%async_computation | async-start | bytes 262144 | tf_op jit(solution)/shard_map/all_to_all | solution.py:190
  21.7 11.7 %all-to-all-done = f32[32,8,128]{2,1,0:T(8,128)S(1)} async-done(((f32[32,8,128]{2,1,0:T(8,128)}), f32[32,8,128]{2,1,0:T(8,128)S(1)}, u32[]{:S(2)}, u32[]{:S(2)}) %all-to-all-start) | async-done | bytes 131104 | tf_op jit(solution)/shard_map/all_to_all | solution.py:190
  34.5 1.5 %collective-permute-start.6 = (bf16[8,8,128]{2,1,0:T(8,128)(2,1)S(1)}, bf16[8,8,128]{2,1,0:T(8,128)(2,1)S(1)}, u32[]{:S(2)}, u32[]{:S(2)}) collective-permute-start(bf16[8,8,128]{2,1,0:T(8,128)(2,1)S(1)} %old_sum.1.o0), channel_id=1, source_target_pairs={{0,1},{1,2},{2,3},{3,0},{4,5},{5,6},{6,7},{7,4},{8,9},{9,10},{10,1... | collective-permute-start | bytes 49160 | tf_op jit(solution)/shard_map/ppermute | solution.py:200
  35.9 2.7 %collective-permute-start.7 = (bf16[8,8,128]{2,1,0:T(8,128)(2,1)S(1)}, bf16[8,8,128]{2,1,0:T(8,128)(2,1)S(1)}, u32[]{:S(2)}, u32[]{:S(2)}) collective-permute-start(bf16[8,8,128]{2,1,0:T(8,128)(2,1)S(1)} %old_sum.1.o0), channel_id=1, source_target_pairs={{0,2},{1,3},{2,0},{3,1},{4,6},{5,7},{6,4},{7,5},{8,10},{9,11},{10,... | collective-permute-start | bytes 49160 | tf_op jit(solution)/shard_map/ppermute | solution.py:200
  38.9 2.9 %collective-permute-start.13 = (bf16[4,16,2048]{2,1,0:T(8,128)(2,1)S(1)}, bf16[4,16,2048]{2,1,0:T(8,128)(2,1)S(1)}, u32[]{:S(2)}, u32[]{:S(2)}) collective-permute-start(bf16[4,16,2048]{2,1,0:T(8,128)(2,1)S(1)} %get-tuple-element.29), channel_id=1, source_target_pairs={{0,2},{1,3},{2,0},{3,1},{4,6},{5,7},{6,4},{7,5},{8,10},{9,11},{10,... | collective-permute-start | bytes 786440 | tf_op jit(solution)/shard_map/ppermute | solution.py:173
  42.4 2.8 %collective-permute-start.14 = (bf16[4,16,2048]{2,1,0:T(8,128)(2,1)S(1)}, bf16[4,16,2048]{2,1,0:T(8,128)(2,1)S(1)}, u32[]{:S(2)}, u32[]{:S(2)}) collective-permute-start(bf16[4,16,2048]{2,1,0:T(8,128)(2,1)S(1)} %get-tuple-element.28), channel_id=1, source_target_pairs={{0,3},{1,0},{2,1},{3,2},{4,7},{5,4},{6,5},{7,6},{8,11},{9,8},{10,9... | collective-permute-start | bytes 786440 | tf_op jit(solution)/shard_map/ppermute | solution.py:173
  45.2 7.2 %collective-permute-done.12 = bf16[4,16,2048]{2,1,0:T(8,128)(2,1)S(1)} collective-permute-done((bf16[4,16,2048]{2,1,0:T(8,128)(2,1)S(1)}, bf16[4,16,2048]{2,1,0:T(8,128)(2,1)S(1)}, u32[]{:S(2)}, u32[]{:S(2)}) %collective-permute-start.12) | collective-permute-done | bytes 262176 | tf_op jit(solution)/shard_map/ppermute | solution.py:173
  52.4 2.1 %collective-permute-done.13 = bf16[4,16,2048]{2,1,0:T(8,128)(2,1)S(1)} collective-permute-done((bf16[4,16,2048]{2,1,0:T(8,128)(2,1)S(1)}, bf16[4,16,2048]{2,1,0:T(8,128)(2,1)S(1)}, u32[]{:S(2)}, u32[]{:S(2)}) %collective-permute-start.13) | collective-permute-done | bytes 262176 | tf_op jit(solution)/shard_map/ppermute | solution.py:173
  55.7 2.7 %collective-permute-start.5 = (bf16[4,16,2048]{2,1,0:T(8,128)(2,1)S(1)}, bf16[4,16,2048]{2,1,0:T(8,128)(2,1)S(1)}, u32[]{:S(2)}, u32[]{:S(2)}) collective-permute-start(bf16[4,16,2048]{2,1,0:T(8,128)(2,1)S(1)} %get-tuple-element.34), channel_id=1, source_target_pairs={{0,3},{1,0},{2,1},{3,2},{4,7},{5,4},{6,5},{7,6},{8,11},{9,8},{10,9... | collective-permute-start | bytes 786440 | tf_op jit(solution)/shard_map/ppermute | solution.py:173
  58.7 6.8 %collective-permute-done.3 = bf16[4,16,2048]{2,1,0:T(8,128)(2,1)S(1)} collective-permute-done((bf16[4,16,2048]{2,1,0:T(8,128)(2,1)S(1)}, bf16[4,16,2048]{2,1,0:T(8,128)(2,1)S(1)}, u32[]{:S(2)}, u32[]{:S(2)}) %collective-permute-start.3) | collective-permute-done | bytes 262176 | tf_op jit(solution)/shard_map/ppermute | solution.py:173
  66.5 1.3 %copy-done.1 = bf16[1,8,64,2048]{3,2,1,0:T(8,128)(2,1)S(1)} copy-done((bf16[1,8,64,2048]{3,2,1,0:T(8,128)(2,1)S(1)}, bf16[1,8,64,2048]{3,2,1,0:T(8,128)(2,1)}, u32[]{:S(2)}) %copy-start.1) | copy-done | bytes 2097176
  67.8 2.9 %first.1 = (bf16[256,2048]{1,0:T(8,128)(2,1)S(1)}, f32[4,256,128]{2,1,0:T(8,128)S(1)}) custom-call(bf16[256,2048]{1,0:T(8,128)(2,1)S(1)} %bitcast.49, bf16[2048,2048]{1,0:T(8,128)(2,1)S(1)} %bitcast.42, bf16[512,2048]{1,0:T(8,128)(2,1)S(1)} %bitcast.45), custom_call_target="tpu_custom_call" | custom-call | tf_op jit(solution)/shard_map/first/pallas_call | solution.py:202
  70.8 4.2 %second.1 = (bf16[256,2048]{1,0:T(8,128)(2,1)S(1)}, bf16[16,32,128]{2,1,0:T(8,128)(2,1)S(1)}, bf16[64,512]{1,0:T(8,128)(2,1)S(1)}) custom-call(s32[34]{0:T(128)S(1)} %pad_add_fusion.meta, bf16[256,2048]{1,0:T(8,128)(2,1)S(1)} %bitcast.48, bf16[2048,2048]{1,0:T(8,128)(2,1)S(1)} %bitcast.43, bf16[512,2048]{1,0:T(8,128)(2,1)S(1)} %bitcast.46, ...), custom_call_target="tpu_custom_call" | custom-call | tf_op jit(solution)/shard_map/second/pallas_call | solution.py:213
  75.0 15.9 %all_to_all.15 = bf16[16,32,128]{2,1,0:T(8,128)(2,1)S(1)} all-to-all(bf16[16,32,128]{2,1,0:T(8,128)(2,1)S(1)} %get-tuple-element.15), channel_id=1, replica_groups=mesh['row'=8,'col'=4,'rhs'=4] {'col','rhs'}, dimensions={0} | all-to-all | bytes 262144 | tf_op jit(solution)/shard_map/all_to_all | solution.py:227
  92.1 4.6 %all-to-all-start.2 = ((bf16[128,32,128]{2,1,0:T(8,128)(2,1)}), bf16[128,32,128]{2,1,0:T(8,128)(2,1)S(1)}, u32[]{:S(2)}, u32[]{:S(2)}) async-start(bf16[128,32,128]{2,1,0:T(8,128)(2,1)} %broadcast_in_dim.48), calls=%async_computation.2 | async-start | bytes 2097152 | tf_op jit(solution)/shard_map/all_to_all | solution.py:229
  96.7 19.0 %all-to-all-done.2 = bf16[128,32,128]{2,1,0:T(8,128)(2,1)S(1)} async-done(((bf16[128,32,128]{2,1,0:T(8,128)(2,1)}), bf16[128,32,128]{2,1,0:T(8,128)(2,1)S(1)}, u32[]{:S(2)}, u32[]{:S(2)}) %all-to-all-start.2) | async-done | bytes 1048608 | tf_op jit(solution)/shard_map/all_to_all | solution.py:229
  115.7 2.1 %sweep.1 = f32[64,2048]{1,0:T(8,128)S(1)} custom-call(s32[34]{0:T(128)S(1)} %pad_add_fusion.meta, s32[8,8]{1,0:T(8,128)S(1)} %copy-done.3, bf16[8,16,32,128]{3,2,1,0:T(8,128)(2,1)S(1)} %bitcast.47, bf16[64,512]{1,0:T(8,128)(2,1)S(1)} %get-tuple-element.16.old_ref, bf16[256,2048]{1,0:T(8,128)(2,1)S(1)} %get-tuple-element.17.x0_ref, ...), custom_call_target="tpu_custom_call" | custom-call | tf_op jit(solution)/shard_map/sweep/pallas_call | solution.py:233
  118.6 1.8 %collective-permute-start.16 = (bf16[16,2048]{1,0:T(8,128)(2,1)S(1)}, bf16[16,2048]{1,0:T(8,128)(2,1)S(1)}, u32[]{:S(2)}, u32[]{:S(2)}) collective-permute-start(bf16[16,2048]{1,0:T(8,128)(2,1)S(1)} %get-tuple-element.39), channel_id=1, source_target_pairs={{0,2},{1,3},{2,0},{3,1},{4,6},{5,7},{6,4},{7,5},{8,10},{9,11},{10,... | collective-permute-start | bytes 196616 | tf_op jit(solution)/shard_map/ppermute | solution.py:246
  121.4 3.1 %collective-permute-done.15 = bf16[16,2048]{1,0:T(8,128)(2,1)S(1)} collective-permute-done((bf16[16,2048]{1,0:T(8,128)(2,1)S(1)}, bf16[16,2048]{1,0:T(8,128)(2,1)S(1)}, u32[]{:S(2)}, u32[]{:S(2)}) %collective-permute-start.15) | collective-permute-done | bytes 65568 | tf_op jit(solution)/shard_map/ppermute | solution.py:246
  (54 shorter events, 13.8 us)
Async XLA Ops:
  0.0 33.4 %copy-start.3 = (s32[8,8]{1,0:T(8,128)S(1)}, s32[8,8]{1,0:T(8,128)}, u32[]{:S(2)}) copy-start(s32[8,8]{1,0:T(8,128)} %ranks.3) | copy-start | bytes 772
  2.1 31.9 %collective-permute-start.10 = (bf16[4,16,2048]{2,1,0:T(8,128)(2,1)S(1)}, bf16[4,16,2048]{2,1,0:T(8,128)(2,1)S(1)}, u32[]{:S(2)}, u32[]{:S(2)}) collective-permute-start(bf16[4,16,2048]{2,1,0:T(8,128)(2,1)S(1)} %get-tuple-element.13), channel_id=1, source_target_pairs={{0,8},{4,12},{8,0},{12,4},{1,9},{5,13},{9,1},{13,5},{2,10},{6,14},... | collective-permute-start | bytes 786440 | tf_op jit(solution)/shard_map/ppermute | solution.py:169
  5.5 28.9 %collective-permute-start.11 = (bf16[4,16,2048]{2,1,0:T(8,128)(2,1)S(1)}, bf16[4,16,2048]{2,1,0:T(8,128)(2,1)S(1)}, u32[]{:S(2)}, u32[]{:S(2)}) collective-permute-start(bf16[4,16,2048]{2,1,0:T(8,128)(2,1)S(1)} %get-tuple-element.13), channel_id=1, source_target_pairs={{0,12},{4,0},{8,4},{12,8},{1,13},{5,1},{9,5},{13,9},{2,14},{6,2},{... | collective-permute-start | bytes 786440 | tf_op jit(solution)/shard_map/ppermute | solution.py:169
  6.6 29.4 %collective-permute-start.9 = (bf16[4,16,2048]{2,1,0:T(8,128)(2,1)S(1)}, bf16[4,16,2048]{2,1,0:T(8,128)(2,1)S(1)}, u32[]{:S(2)}, u32[]{:S(2)}) collective-permute-start(bf16[4,16,2048]{2,1,0:T(8,128)(2,1)S(1)} %get-tuple-element.13), channel_id=1, source_target_pairs={{0,4},{4,8},{8,12},{12,0},{1,5},{5,9},{9,13},{13,1},{2,6},{6,10},{... | collective-permute-start | bytes 786440 | tf_op jit(solution)/shard_map/ppermute | solution.py:169
  7.6 31.2 %collective-permute-start = (bf16[4,16,2048]{2,1,0:T(8,128)(2,1)S(1)}, bf16[4,16,2048]{2,1,0:T(8,128)(2,1)S(1)}, u32[]{:S(2)}, u32[]{:S(2)}) collective-permute-start(bf16[4,16,2048]{2,1,0:T(8,128)(2,1)S(1)} %get-tuple-element.12), channel_id=1, source_target_pairs={{0,4},{4,8},{8,12},{12,0},{1,5},{5,9},{9,13},{13,1},{2,6},{6,10},{... | collective-permute-start | bytes 786440 | tf_op jit(solution)/shard_map/ppermute | solution.py:169
  8.2 30.6 %collective-permute-start.1 = (bf16[4,16,2048]{2,1,0:T(8,128)(2,1)S(1)}, bf16[4,16,2048]{2,1,0:T(8,128)(2,1)S(1)}, u32[]{:S(2)}, u32[]{:S(2)}) collective-permute-start(bf16[4,16,2048]{2,1,0:T(8,128)(2,1)S(1)} %get-tuple-element.12), channel_id=1, source_target_pairs={{0,8},{4,12},{8,0},{12,4},{1,9},{5,13},{9,1},{13,5},{2,10},{6,14},... | collective-permute-start | bytes 786440 | tf_op jit(solution)/shard_map/ppermute | solution.py:169
  15.2 18.2 %all-to-all-start = ((f32[32,8,128]{2,1,0:T(8,128)}), f32[32,8,128]{2,1,0:T(8,128)S(1)}, u32[]{:S(2)}, u32[]{:S(2)}) async-start(f32[32,8,128]{2,1,0:T(8,128)} %bitcast.16), calls=%async_computation | async-start | bytes 262144 | tf_op jit(solution)/shard_map/all_to_all | solution.py:190
  34.0 8.3 %collective-permute-start.2 = (bf16[4,16,2048]{2,1,0:T(8,128)(2,1)S(1)}, bf16[4,16,2048]{2,1,0:T(8,128)(2,1)S(1)}, u32[]{:S(2)}, u32[]{:S(2)}) collective-permute-start(bf16[4,16,2048]{2,1,0:T(8,128)(2,1)S(1)} %get-tuple-element.12), channel_id=1, source_target_pairs={{0,12},{4,0},{8,4},{12,8},{1,13},{5,1},{9,5},{13,9},{2,14},{6,2},{... | collective-permute-start | bytes 786440 | tf_op jit(solution)/shard_map/ppermute | solution.py:169
  34.5 36.3 %collective-permute-start.6 = (bf16[8,8,128]{2,1,0:T(8,128)(2,1)S(1)}, bf16[8,8,128]{2,1,0:T(8,128)(2,1)S(1)}, u32[]{:S(2)}, u32[]{:S(2)}) collective-permute-start(bf16[8,8,128]{2,1,0:T(8,128)(2,1)S(1)} %old_sum.1.o0), channel_id=1, source_target_pairs={{0,1},{1,2},{2,3},{3,0},{4,5},{5,6},{6,7},{7,4},{8,9},{9,10},{10,1... | collective-permute-start | bytes 49160 | tf_op jit(solution)/shard_map/ppermute | solution.py:200
  35.9 34.8 %collective-permute-start.7 = (bf16[8,8,128]{2,1,0:T(8,128)(2,1)S(1)}, bf16[8,8,128]{2,1,0:T(8,128)(2,1)S(1)}, u32[]{:S(2)}, u32[]{:S(2)}) collective-permute-start(bf16[8,8,128]{2,1,0:T(8,128)(2,1)S(1)} %old_sum.1.o0), channel_id=1, source_target_pairs={{0,2},{1,3},{2,0},{3,1},{4,6},{5,7},{6,4},{7,5},{8,10},{9,11},{10,... | collective-permute-start | bytes 49160 | tf_op jit(solution)/shard_map/ppermute | solution.py:200
  38.8 13.7 %collective-permute-start.12 = (bf16[4,16,2048]{2,1,0:T(8,128)(2,1)S(1)}, bf16[4,16,2048]{2,1,0:T(8,128)(2,1)S(1)}, u32[]{:S(2)}, u32[]{:S(2)}) collective-permute-start(bf16[4,16,2048]{2,1,0:T(8,128)(2,1)S(1)} %get-tuple-element.30), channel_id=1, source_target_pairs={{0,1},{1,2},{2,3},{3,0},{4,5},{5,6},{6,7},{7,4},{8,9},{9,10},{10,1... | collective-permute-start | bytes 786440 | tf_op jit(solution)/shard_map/ppermute | solution.py:173
  38.9 15.7 %collective-permute-start.13 = (bf16[4,16,2048]{2,1,0:T(8,128)(2,1)S(1)}, bf16[4,16,2048]{2,1,0:T(8,128)(2,1)S(1)}, u32[]{:S(2)}, u32[]{:S(2)}) collective-permute-start(bf16[4,16,2048]{2,1,0:T(8,128)(2,1)S(1)} %get-tuple-element.29), channel_id=1, source_target_pairs={{0,2},{1,3},{2,0},{3,1},{4,6},{5,7},{6,4},{7,5},{8,10},{9,11},{10,... | collective-permute-start | bytes 786440 | tf_op jit(solution)/shard_map/ppermute | solution.py:173
  42.4 13.4 %collective-permute-start.14 = (bf16[4,16,2048]{2,1,0:T(8,128)(2,1)S(1)}, bf16[4,16,2048]{2,1,0:T(8,128)(2,1)S(1)}, u32[]{:S(2)}, u32[]{:S(2)}) collective-permute-start(bf16[4,16,2048]{2,1,0:T(8,128)(2,1)S(1)} %get-tuple-element.28), channel_id=1, source_target_pairs={{0,3},{1,0},{2,1},{3,2},{4,7},{5,4},{6,5},{7,6},{8,11},{9,8},{10,9... | collective-permute-start | bytes 786440 | tf_op jit(solution)/shard_map/ppermute | solution.py:173
  45.1 21.4 %slice-start = ((s8[8388608]{0:T(1024)(128)(4,1)}), s8[4194304]{0:T(1024)(128)(4,1)S(1)}, s32[]{:S(2)}) async-start(s8[8388608]{0:T(1024)(128)(4,1)} %bitcast.40), calls=%async_computation.3 | async-start | bytes 8388608
  52.4 13.1 %collective-permute-start.3 = (bf16[4,16,2048]{2,1,0:T(8,128)(2,1)S(1)}, bf16[4,16,2048]{2,1,0:T(8,128)(2,1)S(1)}, u32[]{:S(2)}, u32[]{:S(2)}) collective-permute-start(bf16[4,16,2048]{2,1,0:T(8,128)(2,1)S(1)} %get-tuple-element.36), channel_id=1, source_target_pairs={{0,1},{1,2},{2,3},{3,0},{4,5},{5,6},{6,7},{7,4},{8,9},{9,10},{10,1... | collective-permute-start | bytes 786440 | tf_op jit(solution)/shard_map/ppermute | solution.py:173
  54.6 11.0 %collective-permute-start.4 = (bf16[4,16,2048]{2,1,0:T(8,128)(2,1)S(1)}, bf16[4,16,2048]{2,1,0:T(8,128)(2,1)S(1)}, u32[]{:S(2)}, u32[]{:S(2)}) collective-permute-start(bf16[4,16,2048]{2,1,0:T(8,128)(2,1)S(1)} %get-tuple-element.35), channel_id=1, source_target_pairs={{0,2},{1,3},{2,0},{3,1},{4,6},{5,7},{6,4},{7,5},{8,10},{9,11},{10,... | collective-permute-start | bytes 786440 | tf_op jit(solution)/shard_map/ppermute | solution.py:173
  55.7 10.3 %collective-permute-start.5 = (bf16[4,16,2048]{2,1,0:T(8,128)(2,1)S(1)}, bf16[4,16,2048]{2,1,0:T(8,128)(2,1)S(1)}, u32[]{:S(2)}, u32[]{:S(2)}) collective-permute-start(bf16[4,16,2048]{2,1,0:T(8,128)(2,1)S(1)} %get-tuple-element.34), channel_id=1, source_target_pairs={{0,3},{1,0},{2,1},{3,2},{4,7},{5,4},{6,5},{7,6},{8,11},{9,8},{10,9... | collective-permute-start | bytes 786440 | tf_op jit(solution)/shard_map/ppermute | solution.py:173
  58.7 7.8 %slice-start.1 = ((s8[8388608]{0:T(1024)(128)(4,1)}), s8[4194304]{0:T(1024)(128)(4,1)S(1)}, s32[]{:S(2)}) async-start(s8[8388608]{0:T(1024)(128)(4,1)} %bitcast.40), calls=%async_computation.4 | async-start | bytes 8388608
  65.5 5.2 %collective-permute-start.8 = (bf16[8,8,128]{2,1,0:T(8,128)(2,1)S(1)}, bf16[8,8,128]{2,1,0:T(8,128)(2,1)S(1)}, u32[]{:S(2)}, u32[]{:S(2)}) collective-permute-start(bf16[8,8,128]{2,1,0:T(8,128)(2,1)S(1)} %old_sum.1.o0), channel_id=1, source_target_pairs={{0,3},{1,0},{2,1},{3,2},{4,7},{5,4},{6,5},{7,6},{8,11},{9,8},{10,9... | collective-permute-start | bytes 49160 | tf_op jit(solution)/shard_map/ppermute | solution.py:200
  66.2 1.6 %copy-start.1 = (bf16[1,8,64,2048]{3,2,1,0:T(8,128)(2,1)S(1)}, bf16[1,8,64,2048]{3,2,1,0:T(8,128)(2,1)}, u32[]{:S(2)}) copy-start(bf16[1,8,64,2048]{3,2,1,0:T(8,128)(2,1)} %param.11) | copy-start | bytes 6291460
  92.1 23.7 %all-to-all-start.2 = ((bf16[128,32,128]{2,1,0:T(8,128)(2,1)}), bf16[128,32,128]{2,1,0:T(8,128)(2,1)S(1)}, u32[]{:S(2)}, u32[]{:S(2)}) async-start(bf16[128,32,128]{2,1,0:T(8,128)(2,1)} %broadcast_in_dim.48), calls=%async_computation.2 | async-start | bytes 2097152 | tf_op jit(solution)/shard_map/all_to_all | solution.py:229
  117.9 6.6 %collective-permute-start.15 = (bf16[16,2048]{1,0:T(8,128)(2,1)S(1)}, bf16[16,2048]{1,0:T(8,128)(2,1)S(1)}, u32[]{:S(2)}, u32[]{:S(2)}) collective-permute-start(bf16[16,2048]{1,0:T(8,128)(2,1)S(1)} %get-tuple-element.37), channel_id=1, source_target_pairs={{0,1},{1,2},{2,3},{3,0},{4,5},{5,6},{6,7},{7,4},{8,9},{9,10},{10,1... | collective-permute-start | bytes 196616 | tf_op jit(solution)/shard_map/ppermute | solution.py:246
  118.6 5.8 %collective-permute-start.16 = (bf16[16,2048]{1,0:T(8,128)(2,1)S(1)}, bf16[16,2048]{1,0:T(8,128)(2,1)S(1)}, u32[]{:S(2)}, u32[]{:S(2)}) collective-permute-start(bf16[16,2048]{1,0:T(8,128)(2,1)S(1)} %get-tuple-element.39), channel_id=1, source_target_pairs={{0,2},{1,3},{2,0},{3,1},{4,6},{5,7},{6,4},{7,5},{8,10},{9,11},{10,... | collective-permute-start | bytes 196616 | tf_op jit(solution)/shard_map/ppermute | solution.py:246
  120.4 4.6 %collective-permute-start.17 = (bf16[16,2048]{1,0:T(8,128)(2,1)S(1)}, bf16[16,2048]{1,0:T(8,128)(2,1)S(1)}, u32[]{:S(2)}, u32[]{:S(2)}) collective-permute-start(bf16[16,2048]{1,0:T(8,128)(2,1)S(1)} %get-tuple-element.38), channel_id=1, source_target_pairs={{0,3},{1,0},{2,1},{3,2},{4,7},{5,4},{6,5},{7,6},{8,11},{9,8},{10,9... | collective-permute-start | bytes 196616 | tf_op jit(solution)/shard_map/ppermute | solution.py:246
  (2 other events, 2.5 us)

commit v2 on v1

--- a/solution.py
+++ b/solution.py
@@ -168,8 +168,10 @@
         part = parts[n]
         over_col = [part] + [lax.ppermute(part, "col", shift(S, d)) for d in range(1, S)]
         over_rhs = []
+        pieces = tuple(pick(over_col, (q - p - s) % S) for s in range(S))
+        pieces = lax.optimization_barrier(pieces)
         for s in range(S):
-            piece = pick(over_col, (q - p - s) % S)
+            piece = pieces[s]
             over_rhs.append(piece if s == 0 else lax.ppermute(piece, "rhs", shift(S, s)))
         ordered = [pick(over_rhs, (p - x) % S) for x in range(S)]
         halves.append(jnp.stack(ordered, axis=1).reshape(HALF, m))
@@ -207,7 +209,7 @@
             jax.ShapeDtypeStruct((HALF, m), BF),
             jax.ShapeDtypeStruct((4, HALF, 128), F32),
         ],
-        compiler_params=pltpu.CompilerParams(vmem_limit_bytes=20 * 2**20),
+        compiler_params=pltpu.CompilerParams(vmem_limit_bytes=34 * 2**20),
         name="first",
     )(halves[0], inverse[0], right)
     x1, packed, old = pl.pallas_call(
@@ -220,7 +222,7 @@
             jax.ShapeDtypeStruct((R, NB * K), BF),
         ],
         scratch_shapes=[pltpu.VMEM((4, NB * K, 128), F32)],
-        compiler_params=pltpu.CompilerParams(vmem_limit_bytes=22 * 2**20),
+        compiler_params=pltpu.CompilerParams(vmem_limit_bytes=20 * 2**20),
         name="second",
     )(meta, halves[1], inverse[0], right, *packed_old, h0)
 

time: 126 us -> 129 us (1.024)
  local copies, waits for them, and re-layouts: 5.83 us -> 9.23 us
    unnamed x12 -> x10, local copies, waits for them, and re-layouts: 3.83 us -> 7.22 us
where the time goes in v2:
time: 129 us
  waiting for transfers between devices  51.9 us (40%)
  starting transfers between devices  36.8 us (29%)
  blocking collectives  15.9 us (12%)
  Pallas kernels  11.2 us (9%)
  local copies, waits for them, and re-layouts  9.23 us (7%)
  other arithmetic  3.69 us (3%)
    all_to_all x1, waiting for transfers between devices, program(): lax.all_to_all(jnp.broadcast_to(summed[None], (128, 32, 128)), ('row', 'c...  19 us
    ppermute x6, waiting for transfers between devices, program(): lax.ppermute(piece, 'rhs', shift(S, s))  17.1 us
    all_to_all x1, blocking collectives, program(): summed = lax.all_to_all(packed, ('col', 'rhs'), 0, 0, tiled=True)  15.9 us
    all_to_all x1, waiting for transfers between devices, program(): lax.all_to_all(sends.reshape(NB * S, 8, 128), ('row', 'col'), 0, 0, tiled...  11.7 us
    ppermute x6, starting transfers between devices, program(): lax.ppermute(part, 'col', shift(S, d))  9.56 us
    ppermute x6, starting transfers between devices, program(): lax.ppermute(piece, 'rhs', shift(S, s))  9.16 us
    unnamed x10, local copies, waits for them, and re-layouts  7.22 us
    all_to_all x1, starting transfers between devices, program(): lax.all_to_all(sends.reshape(NB * S, 8, 128), ('row', 'col'), 0, 0, tiled...  5.7 us
  transfers between devices with their start and end apart: 20, of which 10 were waited for; matrix products, arithmetic and copies ran while one was open for 1% of the time, Pallas kernels for 4%

profile of v2, /device:TPU:0, one launch (start us, length us, event | category | flops | bytes accessed | tf_op | source)
XLA Modules:
  0.0 129.0 jit_solution(5184593663550211299)
XLA Ops:
  2.1 3.4 %collective-permute-start.10 = (bf16[4,16,2048]{2,1,0:T(8,128)(2,1)S(1)}, bf16[4,16,2048]{2,1,0:T(8,128)(2,1)S(1)}, u32[]{:S(2)}, u32[]{:S(2)}) collective-permute-start(bf16[4,16,2048]{2,1,0:T(8,128)(2,1)S(1)} %get-tuple-element.25), channel_id=1, source_target_pairs={{0,8},{4,12},{8,0},{12,4},{1,9},{5,13},{9,1},{13,5},{2,10},{6,14},... | collective-permute-start | bytes 786440 | tf_op jit(solution)/shard_map/ppermute | solution.py:169
  8.2 3.1 %collective-permute-start.1 = (bf16[4,16,2048]{2,1,0:T(8,128)(2,1)S(1)}, bf16[4,16,2048]{2,1,0:T(8,128)(2,1)S(1)}, u32[]{:S(2)}, u32[]{:S(2)}) collective-permute-start(bf16[4,16,2048]{2,1,0:T(8,128)(2,1)S(1)} %get-tuple-element.20), channel_id=1, source_target_pairs={{0,8},{4,12},{8,0},{12,4},{1,9},{5,13},{9,1},{13,5},{2,10},{6,14},... | collective-permute-start | bytes 786440 | tf_op jit(solution)/shard_map/ppermute | solution.py:169
  11.3 1.6 %copy-done.1 = bf16[1,8,64,2048]{3,2,1,0:T(8,128)(2,1)S(1)} copy-done((bf16[1,8,64,2048]{3,2,1,0:T(8,128)(2,1)S(1)}, bf16[1,8,64,2048]{3,2,1,0:T(8,128)(2,1)}, u32[]{:S(2)}) %copy-start.1) | copy-done | bytes 2097176
  13.8 1.4 %old_send.1 = f32[8,4,8,128]{3,2,1,0:T(8,128)} custom-call(f32[16,2048]{1,0:T(8,128)S(1)} %bitcast.49, bf16[512,2048]{1,0:T(8,128)(2,1)S(1)} %bitcast.42), custom_call_target="tpu_custom_call" | custom-call | tf_op jit(solution)/shard_map/old_send/pallas_call | solution.py:184
  15.2 5.7 %all-to-all-start = ((f32[32,8,128]{2,1,0:T(8,128)}), f32[32,8,128]{2,1,0:T(8,128)S(1)}, u32[]{:S(2)}, u32[]{:S(2)}) async-start(f32[32,8,128]{2,1,0:T(8,128)} %bitcast.16), calls=%async_computation | async-start | bytes 262144 | tf_op jit(solution)/shard_map/all_to_all | solution.py:192
  21.7 11.7 %all-to-all-done = f32[32,8,128]{2,1,0:T(8,128)S(1)} async-done(((f32[32,8,128]{2,1,0:T(8,128)}), f32[32,8,128]{2,1,0:T(8,128)S(1)}, u32[]{:S(2)}, u32[]{:S(2)}) %all-to-all-start) | async-done | bytes 131104 | tf_op jit(solution)/shard_map/all_to_all | solution.py:192
  34.5 1.5 %collective-permute-start.6 = (bf16[8,8,128]{2,1,0:T(8,128)(2,1)S(1)}, bf16[8,8,128]{2,1,0:T(8,128)(2,1)S(1)}, u32[]{:S(2)}, u32[]{:S(2)}) collective-permute-start(bf16[8,8,128]{2,1,0:T(8,128)(2,1)S(1)} %old_sum.1.o0), channel_id=1, source_target_pairs={{0,1},{1,2},{2,3},{3,0},{4,5},{5,6},{6,7},{7,4},{8,9},{9,10},{10,1... | collective-permute-start | bytes 49160 | tf_op jit(solution)/shard_map/ppermute | solution.py:202
  35.9 2.7 %collective-permute-start.7 = (bf16[8,8,128]{2,1,0:T(8,128)(2,1)S(1)}, bf16[8,8,128]{2,1,0:T(8,128)(2,1)S(1)}, u32[]{:S(2)}, u32[]{:S(2)}) collective-permute-start(bf16[8,8,128]{2,1,0:T(8,128)(2,1)S(1)} %old_sum.1.o0), channel_id=1, source_target_pairs={{0,2},{1,3},{2,0},{3,1},{4,6},{5,7},{6,4},{7,5},{8,10},{9,11},{10,... | collective-permute-start | bytes 49160 | tf_op jit(solution)/shard_map/ppermute | solution.py:202
  38.9 2.9 %collective-permute-start.13 = (bf16[4,16,2048]{2,1,0:T(8,128)(2,1)S(1)}, bf16[4,16,2048]{2,1,0:T(8,128)(2,1)S(1)}, u32[]{:S(2)}, u32[]{:S(2)}) collective-permute-start(bf16[4,16,2048]{2,1,0:T(8,128)(2,1)S(1)} %get-tuple-element.28), channel_id=1, source_target_pairs={{0,2},{1,3},{2,0},{3,1},{4,6},{5,7},{6,4},{7,5},{8,10},{9,11},{10,... | collective-permute-start | bytes 786440 | tf_op jit(solution)/shard_map/ppermute | solution.py:175
  42.4 2.8 %collective-permute-start.14 = (bf16[4,16,2048]{2,1,0:T(8,128)(2,1)S(1)}, bf16[4,16,2048]{2,1,0:T(8,128)(2,1)S(1)}, u32[]{:S(2)}, u32[]{:S(2)}) collective-permute-start(bf16[4,16,2048]{2,1,0:T(8,128)(2,1)S(1)} %get-tuple-element.29), channel_id=1, source_target_pairs={{0,3},{1,0},{2,1},{3,2},{4,7},{5,4},{6,5},{7,6},{8,11},{9,8},{10,9... | collective-permute-start | bytes 786440 | tf_op jit(solution)/shard_map/ppermute | solution.py:175
  45.2 7.2 %collective-permute-done.12 = bf16[4,16,2048]{2,1,0:T(8,128)(2,1)S(1)} collective-permute-done((bf16[4,16,2048]{2,1,0:T(8,128)(2,1)S(1)}, bf16[4,16,2048]{2,1,0:T(8,128)(2,1)S(1)}, u32[]{:S(2)}, u32[]{:S(2)}) %collective-permute-start.12) | collective-permute-done | bytes 262176 | tf_op jit(solution)/shard_map/ppermute | solution.py:175
  52.5 2.1 %collective-permute-done.13 = bf16[4,16,2048]{2,1,0:T(8,128)(2,1)S(1)} collective-permute-done((bf16[4,16,2048]{2,1,0:T(8,128)(2,1)S(1)}, bf16[4,16,2048]{2,1,0:T(8,128)(2,1)S(1)}, u32[]{:S(2)}, u32[]{:S(2)}) %collective-permute-start.13) | collective-permute-done | bytes 262176 | tf_op jit(solution)/shard_map/ppermute | solution.py:175
  55.8 2.7 %collective-permute-start.5 = (bf16[4,16,2048]{2,1,0:T(8,128)(2,1)S(1)}, bf16[4,16,2048]{2,1,0:T(8,128)(2,1)S(1)}, u32[]{:S(2)}, u32[]{:S(2)}) collective-permute-start(bf16[4,16,2048]{2,1,0:T(8,128)(2,1)S(1)} %get-tuple-element.24), channel_id=1, source_target_pairs={{0,3},{1,0},{2,1},{3,2},{4,7},{5,4},{6,5},{7,6},{8,11},{9,8},{10,9... | collective-permute-start | bytes 786440 | tf_op jit(solution)/shard_map/ppermute | solution.py:175
  58.7 6.9 %collective-permute-done.3 = bf16[4,16,2048]{2,1,0:T(8,128)(2,1)S(1)} collective-permute-done((bf16[4,16,2048]{2,1,0:T(8,128)(2,1)S(1)}, bf16[4,16,2048]{2,1,0:T(8,128)(2,1)S(1)}, u32[]{:S(2)}, u32[]{:S(2)}) %collective-permute-start.3) | collective-permute-done | bytes 262176 | tf_op jit(solution)/shard_map/ppermute | solution.py:175
  66.4 1.3 %copy-done.2 = bf16[1,8,64,2048]{3,2,1,0:T(8,128)(2,1)S(1)} copy-done((bf16[1,8,64,2048]{3,2,1,0:T(8,128)(2,1)S(1)}, bf16[1,8,64,2048]{3,2,1,0:T(8,128)(2,1)}, u32[]{:S(2)}) %copy-start.2) | copy-done | bytes 2097176
  67.8 3.4 %copy-done = bf16[1,2048,2048]{2,1,0:T(8,128)(2,1)S(1)} copy-done((bf16[1,2048,2048]{2,1,0:T(8,128)(2,1)S(1)}, bf16[1,2048,2048]{2,1,0:T(8,128)(2,1)}, u32[]{:S(2)}) %copy-start) | copy-done | bytes 8388632
  71.2 2.9 %first.1 = (bf16[256,2048]{1,0:T(8,128)(2,1)S(1)}, f32[4,256,128]{2,1,0:T(8,128)S(1)}) custom-call(bf16[256,2048]{1,0:T(8,128)(2,1)S(1)} %bitcast.47, bf16[2048,2048]{1,0:T(8,128)(2,1)S(1)} %bitcast.40, bf16[512,2048]{1,0:T(8,128)(2,1)S(1)} %bitcast.43), custom_call_target="tpu_custom_call" | custom-call | tf_op jit(solution)/shard_map/first/pallas_call | solution.py:204
  74.1 4.2 %second.1 = (bf16[256,2048]{1,0:T(8,128)(2,1)S(1)}, bf16[16,32,128]{2,1,0:T(8,128)(2,1)S(1)}, bf16[64,512]{1,0:T(8,128)(2,1)S(1)}) custom-call(s32[34]{0:T(128)S(1)} %pad_add_fusion.meta, bf16[256,2048]{1,0:T(8,128)(2,1)S(1)} %bitcast.46, bf16[2048,2048]{1,0:T(8,128)(2,1)S(1)} %bitcast.41, bf16[512,2048]{1,0:T(8,128)(2,1)S(1)} %bitcast.44, ...), custom_call_target="tpu_custom_call" | custom-call | tf_op jit(solution)/shard_map/second/pallas_call | solution.py:215
  78.3 15.9 %all_to_all.15 = bf16[16,32,128]{2,1,0:T(8,128)(2,1)S(1)} all-to-all(bf16[16,32,128]{2,1,0:T(8,128)(2,1)S(1)} %get-tuple-element.31), channel_id=1, replica_groups=mesh['row'=8,'col'=4,'rhs'=4] {'col','rhs'}, dimensions={0} | all-to-all | bytes 262144 | tf_op jit(solution)/shard_map/all_to_all | solution.py:229
  95.4 4.6 %all-to-all-start.2 = ((bf16[128,32,128]{2,1,0:T(8,128)(2,1)}), bf16[128,32,128]{2,1,0:T(8,128)(2,1)S(1)}, u32[]{:S(2)}, u32[]{:S(2)}) async-start(bf16[128,32,128]{2,1,0:T(8,128)(2,1)} %broadcast_in_dim.48), calls=%async_computation.2 | async-start | bytes 2097152 | tf_op jit(solution)/shard_map/all_to_all | solution.py:231
  100.0 19.0 %all-to-all-done.2 = bf16[128,32,128]{2,1,0:T(8,128)(2,1)S(1)} async-done(((bf16[128,32,128]{2,1,0:T(8,128)(2,1)}), bf16[128,32,128]{2,1,0:T(8,128)(2,1)S(1)}, u32[]{:S(2)}, u32[]{:S(2)}) %all-to-all-start.2) | async-done | bytes 1048608 | tf_op jit(solution)/shard_map/all_to_all | solution.py:231
  119.0 2.1 %sweep.1 = f32[64,2048]{1,0:T(8,128)S(1)} custom-call(s32[34]{0:T(128)S(1)} %pad_add_fusion.meta, s32[8,8]{1,0:T(8,128)S(1)} %copy-done.4, bf16[8,16,32,128]{3,2,1,0:T(8,128)(2,1)S(1)} %bitcast.45, bf16[64,512]{1,0:T(8,128)(2,1)S(1)} %get-tuple-element.32.old_ref, bf16[256,2048]{1,0:T(8,128)(2,1)S(1)} %get-tuple-element.33.x0_ref, ...), custom_call_target="tpu_custom_call" | custom-call | tf_op jit(solution)/shard_map/sweep/pallas_call | solution.py:235
  121.9 1.8 %collective-permute-start.16 = (bf16[16,2048]{1,0:T(8,128)(2,1)S(1)}, bf16[16,2048]{1,0:T(8,128)(2,1)S(1)}, u32[]{:S(2)}, u32[]{:S(2)}) collective-permute-start(bf16[16,2048]{1,0:T(8,128)(2,1)S(1)} %get-tuple-element.55), channel_id=1, source_target_pairs={{0,2},{1,3},{2,0},{3,1},{4,6},{5,7},{6,4},{7,5},{8,10},{9,11},{10,... | collective-permute-start | bytes 196616 | tf_op jit(solution)/shard_map/ppermute | solution.py:248
  124.7 3.1 %collective-permute-done.15 = bf16[16,2048]{1,0:T(8,128)(2,1)S(1)} collective-permute-done((bf16[16,2048]{1,0:T(8,128)(2,1)S(1)}, bf16[16,2048]{1,0:T(8,128)(2,1)S(1)}, u32[]{:S(2)}, u32[]{:S(2)}) %collective-permute-start.15) | collective-permute-done | bytes 65568 | tf_op jit(solution)/shard_map/ppermute | solution.py:248
  (49 shorter events, 14.9 us)
Async XLA Ops:
  0.0 33.4 %copy-start.4 = (s32[8,8]{1,0:T(8,128)S(1)}, s32[8,8]{1,0:T(8,128)}, u32[]{:S(2)}) copy-start(s32[8,8]{1,0:T(8,128)} %ranks.3) | copy-start | bytes 772
  2.1 31.9 %collective-permute-start.10 = (bf16[4,16,2048]{2,1,0:T(8,128)(2,1)S(1)}, bf16[4,16,2048]{2,1,0:T(8,128)(2,1)S(1)}, u32[]{:S(2)}, u32[]{:S(2)}) collective-permute-start(bf16[4,16,2048]{2,1,0:T(8,128)(2,1)S(1)} %get-tuple-element.25), channel_id=1, source_target_pairs={{0,8},{4,12},{8,0},{12,4},{1,9},{5,13},{9,1},{13,5},{2,10},{6,14},... | collective-permute-start | bytes 786440 | tf_op jit(solution)/shard_map/ppermute | solution.py:169
  5.5 28.9 %collective-permute-start.11 = (bf16[4,16,2048]{2,1,0:T(8,128)(2,1)S(1)}, bf16[4,16,2048]{2,1,0:T(8,128)(2,1)S(1)}, u32[]{:S(2)}, u32[]{:S(2)}) collective-permute-start(bf16[4,16,2048]{2,1,0:T(8,128)(2,1)S(1)} %get-tuple-element.25), channel_id=1, source_target_pairs={{0,12},{4,0},{8,4},{12,8},{1,13},{5,1},{9,5},{13,9},{2,14},{6,2},{... | collective-permute-start | bytes 786440 | tf_op jit(solution)/shard_map/ppermute | solution.py:169
  6.6 29.4 %collective-permute-start.9 = (bf16[4,16,2048]{2,1,0:T(8,128)(2,1)S(1)}, bf16[4,16,2048]{2,1,0:T(8,128)(2,1)S(1)}, u32[]{:S(2)}, u32[]{:S(2)}) collective-permute-start(bf16[4,16,2048]{2,1,0:T(8,128)(2,1)S(1)} %get-tuple-element.25), channel_id=1, source_target_pairs={{0,4},{4,8},{8,12},{12,0},{1,5},{5,9},{9,13},{13,1},{2,6},{6,10},{... | collective-permute-start | bytes 786440 | tf_op jit(solution)/shard_map/ppermute | solution.py:169
  7.6 31.3 %collective-permute-start = (bf16[4,16,2048]{2,1,0:T(8,128)(2,1)S(1)}, bf16[4,16,2048]{2,1,0:T(8,128)(2,1)S(1)}, u32[]{:S(2)}, u32[]{:S(2)}) collective-permute-start(bf16[4,16,2048]{2,1,0:T(8,128)(2,1)S(1)} %get-tuple-element.20), channel_id=1, source_target_pairs={{0,4},{4,8},{8,12},{12,0},{1,5},{5,9},{9,13},{13,1},{2,6},{6,10},{... | collective-permute-start | bytes 786440 | tf_op jit(solution)/shard_map/ppermute | solution.py:169
  8.2 30.7 %collective-permute-start.1 = (bf16[4,16,2048]{2,1,0:T(8,128)(2,1)S(1)}, bf16[4,16,2048]{2,1,0:T(8,128)(2,1)S(1)}, u32[]{:S(2)}, u32[]{:S(2)}) collective-permute-start(bf16[4,16,2048]{2,1,0:T(8,128)(2,1)S(1)} %get-tuple-element.20), channel_id=1, source_target_pairs={{0,8},{4,12},{8,0},{12,4},{1,9},{5,13},{9,1},{13,5},{2,10},{6,14},... | collective-permute-start | bytes 786440 | tf_op jit(solution)/shard_map/ppermute | solution.py:169
  11.3 1.6 %copy-start.1 = (bf16[1,8,64,2048]{3,2,1,0:T(8,128)(2,1)S(1)}, bf16[1,8,64,2048]{3,2,1,0:T(8,128)(2,1)}, u32[]{:S(2)}) copy-start(bf16[1,8,64,2048]{3,2,1,0:T(8,128)(2,1)} %param.11) | copy-start | bytes 6291460
  15.2 18.2 %all-to-all-start = ((f32[32,8,128]{2,1,0:T(8,128)}), f32[32,8,128]{2,1,0:T(8,128)S(1)}, u32[]{:S(2)}, u32[]{:S(2)}) async-start(f32[32,8,128]{2,1,0:T(8,128)} %bitcast.16), calls=%async_computation | async-start | bytes 262144 | tf_op jit(solution)/shard_map/all_to_all | solution.py:192
  34.0 8.3 %collective-permute-start.2 = (bf16[4,16,2048]{2,1,0:T(8,128)(2,1)S(1)}, bf16[4,16,2048]{2,1,0:T(8,128)(2,1)S(1)}, u32[]{:S(2)}, u32[]{:S(2)}) collective-permute-start(bf16[4,16,2048]{2,1,0:T(8,128)(2,1)S(1)} %get-tuple-element.20), channel_id=1, source_target_pairs={{0,12},{4,0},{8,4},{12,8},{1,13},{5,1},{9,5},{13,9},{2,14},{6,2},{... | collective-permute-start | bytes 786440 | tf_op jit(solution)/shard_map/ppermute | solution.py:169
  34.5 39.6 %collective-permute-start.6 = (bf16[8,8,128]{2,1,0:T(8,128)(2,1)S(1)}, bf16[8,8,128]{2,1,0:T(8,128)(2,1)S(1)}, u32[]{:S(2)}, u32[]{:S(2)}) collective-permute-start(bf16[8,8,128]{2,1,0:T(8,128)(2,1)S(1)} %old_sum.1.o0), channel_id=1, source_target_pairs={{0,1},{1,2},{2,3},{3,0},{4,5},{5,6},{6,7},{7,4},{8,9},{9,10},{10,1... | collective-permute-start | bytes 49160 | tf_op jit(solution)/shard_map/ppermute | solution.py:202
  35.9 38.1 %collective-permute-start.7 = (bf16[8,8,128]{2,1,0:T(8,128)(2,1)S(1)}, bf16[8,8,128]{2,1,0:T(8,128)(2,1)S(1)}, u32[]{:S(2)}, u32[]{:S(2)}) collective-permute-start(bf16[8,8,128]{2,1,0:T(8,128)(2,1)S(1)} %old_sum.1.o0), channel_id=1, source_target_pairs={{0,2},{1,3},{2,0},{3,1},{4,6},{5,7},{6,4},{7,5},{8,10},{9,11},{10,... | collective-permute-start | bytes 49160 | tf_op jit(solution)/shard_map/ppermute | solution.py:202
  38.8 13.7 %collective-permute-start.12 = (bf16[4,16,2048]{2,1,0:T(8,128)(2,1)S(1)}, bf16[4,16,2048]{2,1,0:T(8,128)(2,1)S(1)}, u32[]{:S(2)}, u32[]{:S(2)}) collective-permute-start(bf16[4,16,2048]{2,1,0:T(8,128)(2,1)S(1)} %get-tuple-element.27), channel_id=1, source_target_pairs={{0,1},{1,2},{2,3},{3,0},{4,5},{5,6},{6,7},{7,4},{8,9},{9,10},{10,1... | collective-permute-start | bytes 786440 | tf_op jit(solution)/shard_map/ppermute | solution.py:175
  38.9 15.7 %collective-permute-start.13 = (bf16[4,16,2048]{2,1,0:T(8,128)(2,1)S(1)}, bf16[4,16,2048]{2,1,0:T(8,128)(2,1)S(1)}, u32[]{:S(2)}, u32[]{:S(2)}) collective-permute-start(bf16[4,16,2048]{2,1,0:T(8,128)(2,1)S(1)} %get-tuple-element.28), channel_id=1, source_target_pairs={{0,2},{1,3},{2,0},{3,1},{4,6},{5,7},{6,4},{7,5},{8,10},{9,11},{10,... | collective-permute-start | bytes 786440 | tf_op jit(solution)/shard_map/ppermute | solution.py:175
  42.4 13.4 %collective-permute-start.14 = (bf16[4,16,2048]{2,1,0:T(8,128)(2,1)S(1)}, bf16[4,16,2048]{2,1,0:T(8,128)(2,1)S(1)}, u32[]{:S(2)}, u32[]{:S(2)}) collective-permute-start(bf16[4,16,2048]{2,1,0:T(8,128)(2,1)S(1)} %get-tuple-element.29), channel_id=1, source_target_pairs={{0,3},{1,0},{2,1},{3,2},{4,7},{5,4},{6,5},{7,6},{8,11},{9,8},{10,9... | collective-permute-start | bytes 786440 | tf_op jit(solution)/shard_map/ppermute | solution.py:175
  52.5 13.1 %collective-permute-start.3 = (bf16[4,16,2048]{2,1,0:T(8,128)(2,1)S(1)}, bf16[4,16,2048]{2,1,0:T(8,128)(2,1)S(1)}, u32[]{:S(2)}, u32[]{:S(2)}) collective-permute-start(bf16[4,16,2048]{2,1,0:T(8,128)(2,1)S(1)} %get-tuple-element.22), channel_id=1, source_target_pairs={{0,1},{1,2},{2,3},{3,0},{4,5},{5,6},{6,7},{7,4},{8,9},{9,10},{10,1... | collective-permute-start | bytes 786440 | tf_op jit(solution)/shard_map/ppermute | solution.py:175
  54.6 11.0 %collective-permute-start.4 = (bf16[4,16,2048]{2,1,0:T(8,128)(2,1)S(1)}, bf16[4,16,2048]{2,1,0:T(8,128)(2,1)S(1)}, u32[]{:S(2)}, u32[]{:S(2)}) collective-permute-start(bf16[4,16,2048]{2,1,0:T(8,128)(2,1)S(1)} %get-tuple-element.23), channel_id=1, source_target_pairs={{0,2},{1,3},{2,0},{3,1},{4,6},{5,7},{6,4},{7,5},{8,10},{9,11},{10,... | collective-permute-start | bytes 786440 | tf_op jit(solution)/shard_map/ppermute | solution.py:175
  55.8 10.3 %collective-permute-start.5 = (bf16[4,16,2048]{2,1,0:T(8,128)(2,1)S(1)}, bf16[4,16,2048]{2,1,0:T(8,128)(2,1)S(1)}, u32[]{:S(2)}, u32[]{:S(2)}) collective-permute-start(bf16[4,16,2048]{2,1,0:T(8,128)(2,1)S(1)} %get-tuple-element.24), channel_id=1, source_target_pairs={{0,3},{1,0},{2,1},{3,2},{4,7},{5,4},{6,5},{7,6},{8,11},{9,8},{10,9... | collective-permute-start | bytes 786440 | tf_op jit(solution)/shard_map/ppermute | solution.py:175
  65.6 8.5 %collective-permute-start.8 = (bf16[8,8,128]{2,1,0:T(8,128)(2,1)S(1)}, bf16[8,8,128]{2,1,0:T(8,128)(2,1)S(1)}, u32[]{:S(2)}, u32[]{:S(2)}) collective-permute-start(bf16[8,8,128]{2,1,0:T(8,128)(2,1)S(1)} %old_sum.1.o0), channel_id=1, source_target_pairs={{0,3},{1,0},{2,1},{3,2},{4,7},{5,4},{6,5},{7,6},{8,11},{9,8},{10,9... | collective-permute-start | bytes 49160 | tf_op jit(solution)/shard_map/ppermute | solution.py:202
  66.2 1.6 %copy-start.2 = (bf16[1,8,64,2048]{3,2,1,0:T(8,128)(2,1)S(1)}, bf16[1,8,64,2048]{3,2,1,0:T(8,128)(2,1)}, u32[]{:S(2)}) copy-start(bf16[1,8,64,2048]{3,2,1,0:T(8,128)(2,1)} %param.11) | copy-start | bytes 6291460
  67.8 3.4 %copy-start = (bf16[1,2048,2048]{2,1,0:T(8,128)(2,1)S(1)}, bf16[1,2048,2048]{2,1,0:T(8,128)(2,1)}, u32[]{:S(2)}) copy-start(bf16[1,2048,2048]{2,1,0:T(8,128)(2,1)} %param.9) | copy-start | bytes 25165828
  95.4 23.7 %all-to-all-start.2 = ((bf16[128,32,128]{2,1,0:T(8,128)(2,1)}), bf16[128,32,128]{2,1,0:T(8,128)(2,1)S(1)}, u32[]{:S(2)}, u32[]{:S(2)}) async-start(bf16[128,32,128]{2,1,0:T(8,128)(2,1)} %broadcast_in_dim.48), calls=%async_computation.2 | async-start | bytes 2097152 | tf_op jit(solution)/shard_map/all_to_all | solution.py:231
  121.2 6.6 %collective-permute-start.15 = (bf16[16,2048]{1,0:T(8,128)(2,1)S(1)}, bf16[16,2048]{1,0:T(8,128)(2,1)S(1)}, u32[]{:S(2)}, u32[]{:S(2)}) collective-permute-start(bf16[16,2048]{1,0:T(8,128)(2,1)S(1)} %get-tuple-element.53), channel_id=1, source_target_pairs={{0,1},{1,2},{2,3},{3,0},{4,5},{5,6},{6,7},{7,4},{8,9},{9,10},{10,1... | collective-permute-start | bytes 196616 | tf_op jit(solution)/shard_map/ppermute | solution.py:248
  121.9 5.9 %collective-permute-start.16 = (bf16[16,2048]{1,0:T(8,128)(2,1)S(1)}, bf16[16,2048]{1,0:T(8,128)(2,1)S(1)}, u32[]{:S(2)}, u32[]{:S(2)}) collective-permute-start(bf16[16,2048]{1,0:T(8,128)(2,1)S(1)} %get-tuple-element.55), channel_id=1, source_target_pairs={{0,2},{1,3},{2,0},{3,1},{4,6},{5,7},{6,4},{7,5},{8,10},{9,11},{10,... | collective-permute-start | bytes 196616 | tf_op jit(solution)/shard_map/ppermute | solution.py:248
  123.7 4.6 %collective-permute-start.17 = (bf16[16,2048]{1,0:T(8,128)(2,1)S(1)}, bf16[16,2048]{1,0:T(8,128)(2,1)S(1)}, u32[]{:S(2)}, u32[]{:S(2)}) collective-permute-start(bf16[16,2048]{1,0:T(8,128)(2,1)S(1)} %get-tuple-element.54), channel_id=1, source_target_pairs={{0,3},{1,0},{2,1},{3,2},{4,7},{5,4},{6,5},{7,6},{8,11},{9,8},{10,9... | collective-permute-start | bytes 196616 | tf_op jit(solution)/shard_map/ppermute | solution.py:248
  (1 other events, 0.9 us)

commit v3 on v2

--- a/solution.py
+++ b/solution.py
@@ -75,19 +75,17 @@
             old_ref[rows, m * 128 : (m + 1) * 128] = both
 
 
-def first_kernel(a_ref, inv_ref, r_ref, x_ref, h_ref):
+def first_kernel(a_ref, inv_ref, x_ref):
     x_ref[...] = jnp.dot(a_ref[...], inv_ref[...], preferred_element_type=F32).astype(BF)
-    part = nt_dot(x_ref[...], r_ref[...])
-    for m in range(4):
-        h_ref[m] = part[:, m * 128 : (m + 1) * 128]
 
 
 def second_kernel(
-    meta, a_ref, inv_ref, r_ref, o0, o1, o2, o3, h0_ref, x_ref, pack_ref, old_ref, h_s
+    meta, a_ref, inv_ref, r_ref, o0, o1, o2, o3, x0_ref, x_ref, pack_ref, old_ref, h_s
 ):
     unpack_old(meta, (o0, o1, o2, o3), old_ref)
+    part = nt_dot(x0_ref[...], r_ref[...])
     for m in range(4):
-        h_s[m, :HALF] = h0_ref[m]
+        h_s[m, :HALF] = part[:, m * 128 : (m + 1) * 128]
     x_ref[...] = jnp.dot(a_ref[...], inv_ref[...], preferred_element_type=F32).astype(BF)
     part = nt_dot(x_ref[...], r_ref[...])
     for m in range(4):
@@ -201,17 +199,14 @@
     )(meta, ranks, arrived)
     packed_old = [own_old] + [lax.ppermute(own_old, "rhs", shift(S, s)) for s in range(1, S)]
 
-    x0, h0 = pl.pallas_call(
+    x0 = pl.pallas_call(
         first_kernel,
-        in_specs=[vmem] * 3,
-        out_specs=[vmem] * 2,
-        out_shape=[
-            jax.ShapeDtypeStruct((HALF, m), BF),
-            jax.ShapeDtypeStruct((4, HALF, 128), F32),
-        ],
+        in_specs=[vmem] * 2,
+        out_specs=vmem,
+        out_shape=jax.ShapeDtypeStruct((HALF, m), BF),
         compiler_params=pltpu.CompilerParams(vmem_limit_bytes=34 * 2**20),
         name="first",
-    )(halves[0], inverse[0], right)
+    )(halves[0], inverse[0])
     x1, packed, old = pl.pallas_call(
         second_kernel,
         in_specs=[smem] + [vmem] * 8,
@@ -224,7 +219,7 @@
         scratch_shapes=[pltpu.VMEM((4, NB * K, 128), F32)],
         compiler_params=pltpu.CompilerParams(vmem_limit_bytes=20 * 2**20),
         name="second",
-    )(meta, halves[1], inverse[0], right, *packed_old, h0)
+    )(meta, halves[1], inverse[0], right, *packed_old, x0)
 
     summed = lax.all_to_all(packed, ("col", "rhs"), 0, 0, tiled=True)
     summed = summed.astype(F32).sum(axis=0).astype(BF)

time: 129 us -> 128 us (level)
  local copies, waits for them, and re-layouts: 9.23 us -> 7.9 us
    unnamed x10, local copies, waits for them, and re-layouts: 7.22 us -> 5.88 us
  transfers between devices with their start and end apart: 20 -> 20, of which waited for: 10 -> 10; matrix products, arithmetic and copies ran while one was open for 1% -> 1% of each run, Pallas kernels for 4% -> 3%
where the time goes in v3:
time: 128 us
  waiting for transfers between devices  51.9 us (41%)
  starting transfers between devices  36.8 us (29%)
  blocking collectives  15.9 us (12%)
  Pallas kernels  11.3 us (9%)
  local copies, waits for them, and re-layouts  7.9 us (6%)
  other arithmetic  3.69 us (3%)
    all_to_all x1, waiting for transfers between devices, program(): lax.all_to_all(jnp.broadcast_to(summed[None], (128, 32, 128)), ('row', 'c...  19 us
    ppermute x6, waiting for transfers between devices, program(): lax.ppermute(piece, 'rhs', shift(S, s))  17.1 us
    all_to_all x1, blocking collectives, program(): summed = lax.all_to_all(packed, ('col', 'rhs'), 0, 0, tiled=True)  15.9 us
    all_to_all x1, waiting for transfers between devices, program(): lax.all_to_all(sends.reshape(NB * S, 8, 128), ('row', 'col'), 0, 0, tiled...  11.7 us
    ppermute x6, starting transfers between devices, program(): lax.ppermute(part, 'col', shift(S, d))  9.56 us
    ppermute x6, starting transfers between devices, program(): lax.ppermute(piece, 'rhs', shift(S, s))  9.16 us
    unnamed x10, local copies, waits for them, and re-layouts  5.88 us
    all_to_all x1, starting transfers between devices, program(): lax.all_to_all(sends.reshape(NB * S, 8, 128), ('row', 'col'), 0, 0, tiled...  5.7 us
  transfers between devices with their start and end apart: 20, of which 10 were waited for; matrix products, arithmetic and copies ran while one was open for 1% of the time, Pallas kernels for 3%

profile of v3, /device:TPU:0, one launch (start us, length us, event | category | flops | bytes accessed | tf_op | source)
XLA Modules:
  0.0 127.7 jit_solution(12589868540721164705)
XLA Ops:
  0.9 1.2 bitcast_select_fusion
  2.1 3.4 %collective-permute-start.10 = (bf16[4,16,2048]{2,1,0:T(8,128)(2,1)S(1)}, bf16[4,16,2048]{2,1,0:T(8,128)(2,1)S(1)}, u32[]{:S(2)}, u32[]{:S(2)}) collective-permute-start(bf16[4,16,2048]{2,1,0:T(8,128)(2,1)S(1)} %get-tuple-element.23), channel_id=1, source_target_pairs={{0,8},{4,12},{8,0},{12,4},{1,9},{5,13},{9,1},{13,5},{2,10},{6,14},... | collective-permute-start | bytes 786440 | tf_op jit(solution)/shard_map/ppermute | solution.py:167
  8.2 3.1 %collective-permute-start.1 = (bf16[4,16,2048]{2,1,0:T(8,128)(2,1)S(1)}, bf16[4,16,2048]{2,1,0:T(8,128)(2,1)S(1)}, u32[]{:S(2)}, u32[]{:S(2)}) collective-permute-start(bf16[4,16,2048]{2,1,0:T(8,128)(2,1)S(1)} %get-tuple-element.18), channel_id=1, source_target_pairs={{0,8},{4,12},{8,0},{12,4},{1,9},{5,13},{9,1},{13,5},{2,10},{6,14},... | collective-permute-start | bytes 786440 | tf_op jit(solution)/shard_map/ppermute | solution.py:167
  11.3 1.6 %copy-done.1 = bf16[1,8,64,2048]{3,2,1,0:T(8,128)(2,1)S(1)} copy-done((bf16[1,8,64,2048]{3,2,1,0:T(8,128)(2,1)S(1)}, bf16[1,8,64,2048]{3,2,1,0:T(8,128)(2,1)}, u32[]{:S(2)}) %copy-start.1) | copy-done | bytes 2097176
  13.8 1.4 %old_send.1 = f32[8,4,8,128]{3,2,1,0:T(8,128)} custom-call(f32[16,2048]{1,0:T(8,128)S(1)} %bitcast.48, bf16[512,2048]{1,0:T(8,128)(2,1)S(1)} %bitcast.42), custom_call_target="tpu_custom_call" | custom-call | tf_op jit(solution)/shard_map/old_send/pallas_call | solution.py:182
  15.2 5.7 %all-to-all-start = ((f32[32,8,128]{2,1,0:T(8,128)}), f32[32,8,128]{2,1,0:T(8,128)S(1)}, u32[]{:S(2)}, u32[]{:S(2)}) async-start(f32[32,8,128]{2,1,0:T(8,128)} %bitcast.16), calls=%async_computation | async-start | bytes 262144 | tf_op jit(solution)/shard_map/all_to_all | solution.py:190
  21.7 11.7 %all-to-all-done = f32[32,8,128]{2,1,0:T(8,128)S(1)} async-done(((f32[32,8,128]{2,1,0:T(8,128)}), f32[32,8,128]{2,1,0:T(8,128)S(1)}, u32[]{:S(2)}, u32[]{:S(2)}) %all-to-all-start) | async-done | bytes 131104 | tf_op jit(solution)/shard_map/all_to_all | solution.py:190
  34.5 1.5 %collective-permute-start.6 = (bf16[8,8,128]{2,1,0:T(8,128)(2,1)S(1)}, bf16[8,8,128]{2,1,0:T(8,128)(2,1)S(1)}, u32[]{:S(2)}, u32[]{:S(2)}) collective-permute-start(bf16[8,8,128]{2,1,0:T(8,128)(2,1)S(1)} %old_sum.1.o0), channel_id=1, source_target_pairs={{0,1},{1,2},{2,3},{3,0},{4,5},{5,6},{6,7},{7,4},{8,9},{9,10},{10,1... | collective-permute-start | bytes 49160 | tf_op jit(solution)/shard_map/ppermute | solution.py:200
  35.9 2.7 %collective-permute-start.7 = (bf16[8,8,128]{2,1,0:T(8,128)(2,1)S(1)}, bf16[8,8,128]{2,1,0:T(8,128)(2,1)S(1)}, u32[]{:S(2)}, u32[]{:S(2)}) collective-permute-start(bf16[8,8,128]{2,1,0:T(8,128)(2,1)S(1)} %old_sum.1.o0), channel_id=1, source_target_pairs={{0,2},{1,3},{2,0},{3,1},{4,6},{5,7},{6,4},{7,5},{8,10},{9,11},{10,... | collective-permute-start | bytes 49160 | tf_op jit(solution)/shard_map/ppermute | solution.py:200
  38.9 2.9 %collective-permute-start.13 = (bf16[4,16,2048]{2,1,0:T(8,128)(2,1)S(1)}, bf16[4,16,2048]{2,1,0:T(8,128)(2,1)S(1)}, u32[]{:S(2)}, u32[]{:S(2)}) collective-permute-start(bf16[4,16,2048]{2,1,0:T(8,128)(2,1)S(1)} %get-tuple-element.26), channel_id=1, source_target_pairs={{0,2},{1,3},{2,0},{3,1},{4,6},{5,7},{6,4},{7,5},{8,10},{9,11},{10,... | collective-permute-start | bytes 786440 | tf_op jit(solution)/shard_map/ppermute | solution.py:173
  42.4 2.8 %collective-permute-start.14 = (bf16[4,16,2048]{2,1,0:T(8,128)(2,1)S(1)}, bf16[4,16,2048]{2,1,0:T(8,128)(2,1)S(1)}, u32[]{:S(2)}, u32[]{:S(2)}) collective-permute-start(bf16[4,16,2048]{2,1,0:T(8,128)(2,1)S(1)} %get-tuple-element.27), channel_id=1, source_target_pairs={{0,3},{1,0},{2,1},{3,2},{4,7},{5,4},{6,5},{7,6},{8,11},{9,8},{10,9... | collective-permute-start | bytes 786440 | tf_op jit(solution)/shard_map/ppermute | solution.py:173
  45.2 7.2 %collective-permute-done.12 = bf16[4,16,2048]{2,1,0:T(8,128)(2,1)S(1)} collective-permute-done((bf16[4,16,2048]{2,1,0:T(8,128)(2,1)S(1)}, bf16[4,16,2048]{2,1,0:T(8,128)(2,1)S(1)}, u32[]{:S(2)}, u32[]{:S(2)}) %collective-permute-start.12) | collective-permute-done | bytes 262176 | tf_op jit(solution)/shard_map/ppermute | solution.py:173
  52.5 2.1 %collective-permute-done.13 = bf16[4,16,2048]{2,1,0:T(8,128)(2,1)S(1)} collective-permute-done((bf16[4,16,2048]{2,1,0:T(8,128)(2,1)S(1)}, bf16[4,16,2048]{2,1,0:T(8,128)(2,1)S(1)}, u32[]{:S(2)}, u32[]{:S(2)}) %collective-permute-start.13) | collective-permute-done | bytes 262176 | tf_op jit(solution)/shard_map/ppermute | solution.py:173
  55.8 2.7 %collective-permute-start.5 = (bf16[4,16,2048]{2,1,0:T(8,128)(2,1)S(1)}, bf16[4,16,2048]{2,1,0:T(8,128)(2,1)S(1)}, u32[]{:S(2)}, u32[]{:S(2)}) collective-permute-start(bf16[4,16,2048]{2,1,0:T(8,128)(2,1)S(1)} %get-tuple-element.22), channel_id=1, source_target_pairs={{0,3},{1,0},{2,1},{3,2},{4,7},{5,4},{6,5},{7,6},{8,11},{9,8},{10,9... | collective-permute-start | bytes 786440 | tf_op jit(solution)/shard_map/ppermute | solution.py:173
  58.7 6.9 %collective-permute-done.3 = bf16[4,16,2048]{2,1,0:T(8,128)(2,1)S(1)} collective-permute-done((bf16[4,16,2048]{2,1,0:T(8,128)(2,1)S(1)}, bf16[4,16,2048]{2,1,0:T(8,128)(2,1)S(1)}, u32[]{:S(2)}, u32[]{:S(2)}) %collective-permute-start.3) | collective-permute-done | bytes 262176 | tf_op jit(solution)/shard_map/ppermute | solution.py:173
  66.4 3.4 %copy-done = bf16[1,2048,2048]{2,1,0:T(8,128)(2,1)S(1)} copy-done((bf16[1,2048,2048]{2,1,0:T(8,128)(2,1)S(1)}, bf16[1,2048,2048]{2,1,0:T(8,128)(2,1)}, u32[]{:S(2)}) %copy-start) | copy-done | bytes 8388632
  69.8 2.3 %first.1.x0_ref = bf16[256,2048]{1,0:T(8,128)(2,1)S(1)} custom-call(bf16[256,2048]{1,0:T(8,128)(2,1)S(1)} %bitcast.46, bf16[2048,2048]{1,0:T(8,128)(2,1)S(1)} %bitcast.40), custom_call_target="tpu_custom_call" | custom-call | tf_op jit(solution)/shard_map/first/pallas_call | solution.py:202
  72.2 4.8 %second.1 = (bf16[256,2048]{1,0:T(8,128)(2,1)S(1)}, bf16[16,32,128]{2,1,0:T(8,128)(2,1)S(1)}, bf16[64,512]{1,0:T(8,128)(2,1)S(1)}) custom-call(s32[34]{0:T(128)S(1)} %pad_add_fusion.meta, bf16[256,2048]{1,0:T(8,128)(2,1)S(1)} %bitcast.45, bf16[2048,2048]{1,0:T(8,128)(2,1)S(1)} %bitcast.41, bf16[512,2048]{1,0:T(8,128)(2,1)S(1)} %bitcast.43, ...), custom_call_target="tpu_custom_call" | custom-call | tf_op jit(solution)/shard_map/second/pallas_call | solution.py:210
  77.0 15.9 %all_to_all.15 = bf16[16,32,128]{2,1,0:T(8,128)(2,1)S(1)} all-to-all(bf16[16,32,128]{2,1,0:T(8,128)(2,1)S(1)} %get-tuple-element.28), channel_id=1, replica_groups=mesh['row'=8,'col'=4,'rhs'=4] {'col','rhs'}, dimensions={0} | all-to-all | bytes 262144 | tf_op jit(solution)/shard_map/all_to_all | solution.py:224
  94.1 4.6 %all-to-all-start.2 = ((bf16[128,32,128]{2,1,0:T(8,128)(2,1)}), bf16[128,32,128]{2,1,0:T(8,128)(2,1)S(1)}, u32[]{:S(2)}, u32[]{:S(2)}) async-start(bf16[128,32,128]{2,1,0:T(8,128)(2,1)} %broadcast_in_dim.48), calls=%async_computation.2 | async-start | bytes 2097152 | tf_op jit(solution)/shard_map/all_to_all | solution.py:226
  98.8 19.0 %all-to-all-done.2 = bf16[128,32,128]{2,1,0:T(8,128)(2,1)S(1)} async-done(((bf16[128,32,128]{2,1,0:T(8,128)(2,1)}), bf16[128,32,128]{2,1,0:T(8,128)(2,1)S(1)}, u32[]{:S(2)}, u32[]{:S(2)}) %all-to-all-start.2) | async-done | bytes 1048608 | tf_op jit(solution)/shard_map/all_to_all | solution.py:226
  117.7 2.1 %sweep.1 = f32[64,2048]{1,0:T(8,128)S(1)} custom-call(s32[34]{0:T(128)S(1)} %pad_add_fusion.meta, s32[8,8]{1,0:T(8,128)S(1)} %copy-done.4, bf16[8,16,32,128]{3,2,1,0:T(8,128)(2,1)S(1)} %bitcast.44, bf16[64,512]{1,0:T(8,128)(2,1)S(1)} %get-tuple-element.29.old_ref, bf16[256,2048]{1,0:T(8,128)(2,1)S(1)} %first.1.x0_ref, ...), custom_call_target="tpu_custom_call" | custom-call | tf_op jit(solution)/shard_map/sweep/pallas_call | solution.py:230
  120.6 1.8 %collective-permute-start.16 = (bf16[16,2048]{1,0:T(8,128)(2,1)S(1)}, bf16[16,2048]{1,0:T(8,128)(2,1)S(1)}, u32[]{:S(2)}, u32[]{:S(2)}) collective-permute-start(bf16[16,2048]{1,0:T(8,128)(2,1)S(1)} %get-tuple-element.51), channel_id=1, source_target_pairs={{0,2},{1,3},{2,0},{3,1},{4,6},{5,7},{6,4},{7,5},{8,10},{9,11},{10,... | collective-permute-start | bytes 196616 | tf_op jit(solution)/shard_map/ppermute | solution.py:243
  123.4 3.1 %collective-permute-done.15 = bf16[16,2048]{1,0:T(8,128)(2,1)S(1)} collective-permute-done((bf16[16,2048]{1,0:T(8,128)(2,1)S(1)}, bf16[16,2048]{1,0:T(8,128)(2,1)S(1)}, u32[]{:S(2)}, u32[]{:S(2)}) %collective-permute-start.15) | collective-permute-done | bytes 65568 | tf_op jit(solution)/shard_map/ppermute | solution.py:243
  (49 shorter events, 13.7 us)
Async XLA Ops:
  0.0 33.4 %copy-start.4 = (s32[8,8]{1,0:T(8,128)S(1)}, s32[8,8]{1,0:T(8,128)}, u32[]{:S(2)}) copy-start(s32[8,8]{1,0:T(8,128)} %ranks.3) | copy-start | bytes 772
  2.1 31.9 %collective-permute-start.10 = (bf16[4,16,2048]{2,1,0:T(8,128)(2,1)S(1)}, bf16[4,16,2048]{2,1,0:T(8,128)(2,1)S(1)}, u32[]{:S(2)}, u32[]{:S(2)}) collective-permute-start(bf16[4,16,2048]{2,1,0:T(8,128)(2,1)S(1)} %get-tuple-element.23), channel_id=1, source_target_pairs={{0,8},{4,12},{8,0},{12,4},{1,9},{5,13},{9,1},{13,5},{2,10},{6,14},... | collective-permute-start | bytes 786440 | tf_op jit(solution)/shard_map/ppermute | solution.py:167
  5.5 28.9 %collective-permute-start.11 = (bf16[4,16,2048]{2,1,0:T(8,128)(2,1)S(1)}, bf16[4,16,2048]{2,1,0:T(8,128)(2,1)S(1)}, u32[]{:S(2)}, u32[]{:S(2)}) collective-permute-start(bf16[4,16,2048]{2,1,0:T(8,128)(2,1)S(1)} %get-tuple-element.23), channel_id=1, source_target_pairs={{0,12},{4,0},{8,4},{12,8},{1,13},{5,1},{9,5},{13,9},{2,14},{6,2},{... | collective-permute-start | bytes 786440 | tf_op jit(solution)/shard_map/ppermute | solution.py:167
  6.6 29.4 %collective-permute-start.9 = (bf16[4,16,2048]{2,1,0:T(8,128)(2,1)S(1)}, bf16[4,16,2048]{2,1,0:T(8,128)(2,1)S(1)}, u32[]{:S(2)}, u32[]{:S(2)}) collective-permute-start(bf16[4,16,2048]{2,1,0:T(8,128)(2,1)S(1)} %get-tuple-element.23), channel_id=1, source_target_pairs={{0,4},{4,8},{8,12},{12,0},{1,5},{5,9},{9,13},{13,1},{2,6},{6,10},{... | collective-permute-start | bytes 786440 | tf_op jit(solution)/shard_map/ppermute | solution.py:167
  7.6 31.3 %collective-permute-start = (bf16[4,16,2048]{2,1,0:T(8,128)(2,1)S(1)}, bf16[4,16,2048]{2,1,0:T(8,128)(2,1)S(1)}, u32[]{:S(2)}, u32[]{:S(2)}) collective-permute-start(bf16[4,16,2048]{2,1,0:T(8,128)(2,1)S(1)} %get-tuple-element.18), channel_id=1, source_target_pairs={{0,4},{4,8},{8,12},{12,0},{1,5},{5,9},{9,13},{13,1},{2,6},{6,10},{... | collective-permute-start | bytes 786440 | tf_op jit(solution)/shard_map/ppermute | solution.py:167
  8.2 30.7 %collective-permute-start.1 = (bf16[4,16,2048]{2,1,0:T(8,128)(2,1)S(1)}, bf16[4,16,2048]{2,1,0:T(8,128)(2,1)S(1)}, u32[]{:S(2)}, u32[]{:S(2)}) collective-permute-start(bf16[4,16,2048]{2,1,0:T(8,128)(2,1)S(1)} %get-tuple-element.18), channel_id=1, source_target_pairs={{0,8},{4,12},{8,0},{12,4},{1,9},{5,13},{9,1},{13,5},{2,10},{6,14},... | collective-permute-start | bytes 786440 | tf_op jit(solution)/shard_map/ppermute | solution.py:167
  11.3 1.6 %copy-start.1 = (bf16[1,8,64,2048]{3,2,1,0:T(8,128)(2,1)S(1)}, bf16[1,8,64,2048]{3,2,1,0:T(8,128)(2,1)}, u32[]{:S(2)}) copy-start(bf16[1,8,64,2048]{3,2,1,0:T(8,128)(2,1)} %param.11) | copy-start | bytes 6291460
  15.2 18.2 %all-to-all-start = ((f32[32,8,128]{2,1,0:T(8,128)}), f32[32,8,128]{2,1,0:T(8,128)S(1)}, u32[]{:S(2)}, u32[]{:S(2)}) async-start(f32[32,8,128]{2,1,0:T(8,128)} %bitcast.16), calls=%async_computation | async-start | bytes 262144 | tf_op jit(solution)/shard_map/all_to_all | solution.py:190
  34.0 8.3 %collective-permute-start.2 = (bf16[4,16,2048]{2,1,0:T(8,128)(2,1)S(1)}, bf16[4,16,2048]{2,1,0:T(8,128)(2,1)S(1)}, u32[]{:S(2)}, u32[]{:S(2)}) collective-permute-start(bf16[4,16,2048]{2,1,0:T(8,128)(2,1)S(1)} %get-tuple-element.18), channel_id=1, source_target_pairs={{0,12},{4,0},{8,4},{12,8},{1,13},{5,1},{9,5},{13,9},{2,14},{6,2},{... | collective-permute-start | bytes 786440 | tf_op jit(solution)/shard_map/ppermute | solution.py:167
  34.5 37.7 %collective-permute-start.6 = (bf16[8,8,128]{2,1,0:T(8,128)(2,1)S(1)}, bf16[8,8,128]{2,1,0:T(8,128)(2,1)S(1)}, u32[]{:S(2)}, u32[]{:S(2)}) collective-permute-start(bf16[8,8,128]{2,1,0:T(8,128)(2,1)S(1)} %old_sum.1.o0), channel_id=1, source_target_pairs={{0,1},{1,2},{2,3},{3,0},{4,5},{5,6},{6,7},{7,4},{8,9},{9,10},{10,1... | collective-permute-start | bytes 49160 | tf_op jit(solution)/shard_map/ppermute | solution.py:200
  35.9 36.2 %collective-permute-start.7 = (bf16[8,8,128]{2,1,0:T(8,128)(2,1)S(1)}, bf16[8,8,128]{2,1,0:T(8,128)(2,1)S(1)}, u32[]{:S(2)}, u32[]{:S(2)}) collective-permute-start(bf16[8,8,128]{2,1,0:T(8,128)(2,1)S(1)} %old_sum.1.o0), channel_id=1, source_target_pairs={{0,2},{1,3},{2,0},{3,1},{4,6},{5,7},{6,4},{7,5},{8,10},{9,11},{10,... | collective-permute-start | bytes 49160 | tf_op jit(solution)/shard_map/ppermute | solution.py:200
  38.8 13.7 %collective-permute-start.12 = (bf16[4,16,2048]{2,1,0:T(8,128)(2,1)S(1)}, bf16[4,16,2048]{2,1,0:T(8,128)(2,1)S(1)}, u32[]{:S(2)}, u32[]{:S(2)}) collective-permute-start(bf16[4,16,2048]{2,1,0:T(8,128)(2,1)S(1)} %get-tuple-element.25), channel_id=1, source_target_pairs={{0,1},{1,2},{2,3},{3,0},{4,5},{5,6},{6,7},{7,4},{8,9},{9,10},{10,1... | collective-permute-start | bytes 786440 | tf_op jit(solution)/shard_map/ppermute | solution.py:173
  38.9 15.7 %collective-permute-start.13 = (bf16[4,16,2048]{2,1,0:T(8,128)(2,1)S(1)}, bf16[4,16,2048]{2,1,0:T(8,128)(2,1)S(1)}, u32[]{:S(2)}, u32[]{:S(2)}) collective-permute-start(bf16[4,16,2048]{2,1,0:T(8,128)(2,1)S(1)} %get-tuple-element.26), channel_id=1, source_target_pairs={{0,2},{1,3},{2,0},{3,1},{4,6},{5,7},{6,4},{7,5},{8,10},{9,11},{10,... | collective-permute-start | bytes 786440 | tf_op jit(solution)/shard_map/ppermute | solution.py:173
  42.4 13.4 %collective-permute-start.14 = (bf16[4,16,2048]{2,1,0:T(8,128)(2,1)S(1)}, bf16[4,16,2048]{2,1,0:T(8,128)(2,1)S(1)}, u32[]{:S(2)}, u32[]{:S(2)}) collective-permute-start(bf16[4,16,2048]{2,1,0:T(8,128)(2,1)S(1)} %get-tuple-element.27), channel_id=1, source_target_pairs={{0,3},{1,0},{2,1},{3,2},{4,7},{5,4},{6,5},{7,6},{8,11},{9,8},{10,9... | collective-permute-start | bytes 786440 | tf_op jit(solution)/shard_map/ppermute | solution.py:173
  52.5 13.1 %collective-permute-start.3 = (bf16[4,16,2048]{2,1,0:T(8,128)(2,1)S(1)}, bf16[4,16,2048]{2,1,0:T(8,128)(2,1)S(1)}, u32[]{:S(2)}, u32[]{:S(2)}) collective-permute-start(bf16[4,16,2048]{2,1,0:T(8,128)(2,1)S(1)} %get-tuple-element.20), channel_id=1, source_target_pairs={{0,1},{1,2},{2,3},{3,0},{4,5},{5,6},{6,7},{7,4},{8,9},{9,10},{10,1... | collective-permute-start | bytes 786440 | tf_op jit(solution)/shard_map/ppermute | solution.py:173
  54.6 11.0 %collective-permute-start.4 = (bf16[4,16,2048]{2,1,0:T(8,128)(2,1)S(1)}, bf16[4,16,2048]{2,1,0:T(8,128)(2,1)S(1)}, u32[]{:S(2)}, u32[]{:S(2)}) collective-permute-start(bf16[4,16,2048]{2,1,0:T(8,128)(2,1)S(1)} %get-tuple-element.21), channel_id=1, source_target_pairs={{0,2},{1,3},{2,0},{3,1},{4,6},{5,7},{6,4},{7,5},{8,10},{9,11},{10,... | collective-permute-start | bytes 786440 | tf_op jit(solution)/shard_map/ppermute | solution.py:173
  55.8 10.3 %collective-permute-start.5 = (bf16[4,16,2048]{2,1,0:T(8,128)(2,1)S(1)}, bf16[4,16,2048]{2,1,0:T(8,128)(2,1)S(1)}, u32[]{:S(2)}, u32[]{:S(2)}) collective-permute-start(bf16[4,16,2048]{2,1,0:T(8,128)(2,1)S(1)} %get-tuple-element.22), channel_id=1, source_target_pairs={{0,3},{1,0},{2,1},{3,2},{4,7},{5,4},{6,5},{7,6},{8,11},{9,8},{10,9... | collective-permute-start | bytes 786440 | tf_op jit(solution)/shard_map/ppermute | solution.py:173
  65.6 6.6 %collective-permute-start.8 = (bf16[8,8,128]{2,1,0:T(8,128)(2,1)S(1)}, bf16[8,8,128]{2,1,0:T(8,128)(2,1)S(1)}, u32[]{:S(2)}, u32[]{:S(2)}) collective-permute-start(bf16[8,8,128]{2,1,0:T(8,128)(2,1)S(1)} %old_sum.1.o0), channel_id=1, source_target_pairs={{0,3},{1,0},{2,1},{3,2},{4,7},{5,4},{6,5},{7,6},{8,11},{9,8},{10,9... | collective-permute-start | bytes 49160 | tf_op jit(solution)/shard_map/ppermute | solution.py:200
  66.4 3.4 %copy-start = (bf16[1,2048,2048]{2,1,0:T(8,128)(2,1)S(1)}, bf16[1,2048,2048]{2,1,0:T(8,128)(2,1)}, u32[]{:S(2)}) copy-start(bf16[1,2048,2048]{2,1,0:T(8,128)(2,1)} %param.9) | copy-start | bytes 25165828
  69.8 2.4 %copy-start.2 = (bf16[1,8,64,2048]{3,2,1,0:T(8,128)(2,1)S(1)}, bf16[1,8,64,2048]{3,2,1,0:T(8,128)(2,1)}, u32[]{:S(2)}) copy-start(bf16[1,8,64,2048]{3,2,1,0:T(8,128)(2,1)} %param.11) | copy-start | bytes 6291460
  94.1 23.7 %all-to-all-start.2 = ((bf16[128,32,128]{2,1,0:T(8,128)(2,1)}), bf16[128,32,128]{2,1,0:T(8,128)(2,1)S(1)}, u32[]{:S(2)}, u32[]{:S(2)}) async-start(bf16[128,32,128]{2,1,0:T(8,128)(2,1)} %broadcast_in_dim.48), calls=%async_computation.2 | async-start | bytes 2097152 | tf_op jit(solution)/shard_map/all_to_all | solution.py:226
  119.9 6.6 %collective-permute-start.15 = (bf16[16,2048]{1,0:T(8,128)(2,1)S(1)}, bf16[16,2048]{1,0:T(8,128)(2,1)S(1)}, u32[]{:S(2)}, u32[]{:S(2)}) collective-permute-start(bf16[16,2048]{1,0:T(8,128)(2,1)S(1)} %get-tuple-element.49), channel_id=1, source_target_pairs={{0,1},{1,2},{2,3},{3,0},{4,5},{5,6},{6,7},{7,4},{8,9},{9,10},{10,1... | collective-permute-start | bytes 196616 | tf_op jit(solution)/shard_map/ppermute | solution.py:243
  120.6 5.9 %collective-permute-start.16 = (bf16[16,2048]{1,0:T(8,128)(2,1)S(1)}, bf16[16,2048]{1,0:T(8,128)(2,1)S(1)}, u32[]{:S(2)}, u32[]{:S(2)}) collective-permute-start(bf16[16,2048]{1,0:T(8,128)(2,1)S(1)} %get-tuple-element.51), channel_id=1, source_target_pairs={{0,2},{1,3},{2,0},{3,1},{4,6},{5,7},{6,4},{7,5},{8,10},{9,11},{10,... | collective-permute-start | bytes 196616 | tf_op jit(solution)/shard_map/ppermute | solution.py:243
  122.5 4.6 %collective-permute-start.17 = (bf16[16,2048]{1,0:T(8,128)(2,1)S(1)}, bf16[16,2048]{1,0:T(8,128)(2,1)S(1)}, u32[]{:S(2)}, u32[]{:S(2)}) collective-permute-start(bf16[16,2048]{1,0:T(8,128)(2,1)S(1)} %get-tuple-element.50), channel_id=1, source_target_pairs={{0,3},{1,0},{2,1},{3,2},{4,7},{5,4},{6,5},{7,6},{8,11},{9,8},{10,9... | collective-permute-start | bytes 196616 | tf_op jit(solution)/shard_map/ppermute | solution.py:243
  (1 other events, 0.9 us)
